TPU v7x, 32 devices: a whole 2x2x4 slice. The times are simulated.
32 devices in a mesh: seq: 32 (over z, y, x, core).
Axes of the slice: x: 2, y: 2, z: 4, core: 2. Of those that a mesh axis runs over, the one named last changes fastest.
Arguments:
- queries: bfloat16 [2, 8, 8192], replicated, may hold values from -4 to 4, as said below
- kv_pages: bfloat16 [8192, 4, 2, 1024], P('seq'), may hold values from -448 to 448
- page_scales: bfloat16 [8192, 32], P('seq'), may hold values from 0.39 to 4.02
- page_owner: int32 [8192], P('seq'), may hold values from 0 to 31, as said below
- valid_pages: int32 [32], P('seq'), may hold values from 192 to 256, as said below
- branch_kv: bfloat16 [2, 2, 8, 1024], replicated, may hold values from -128 to 128
- parents: int32 [8], replicated, may hold values from 0 to 7
Outputs:
- page_cache: bfloat16 [8192, 4, 2, 1024], P('seq')
- cache_scales: bfloat16 [8192, 32], P('seq')
- attended: float32 [2, 8, 8192], replicated
Inputs may be any that keep to these rules, and one draw needn't show every extreme that they name: `queries`: within the range printed. page_owner[p] may be any device; at most 8 pages of one shard share an owner, and some shard sends 8 live pages to one owner; at most 256 live pages share an owner, and one owner has exactly 256. `valid_pages`: some shard has all 256 pages live.
All inputs are finite; a program needn't handle non-finite values.
Results may differ from a plain program's by a relative error of at most 0.001.
Values may be sent and summed in bfloat16 or wider, within the bound.
No kernel may reach another device: no remote copies, remote signals or barrier semaphores. Data moves between devices by JAX's collectives and lax.ppermute only.
A program may use at most 128 MiB of HBM per device.

v0:
```python
import math

import jax
import jax.numpy as jnp
from jax import lax
from jax.sharding import PartitionSpec as P

HQ = 64
KEY_VALUE_HEADS = 8
HEAD_SIZE = 128
LAYERS = 2
BEAMS = 8
PAGE = 2


def combined_all(shard, axis, combine):
    everything = jax.tree.map(lambda part: lax.all_gather(part, axis), shard)
    initial = jax.tree.map(lambda part: part[0], everything)

    def lap(k, so_far):
        return combine(so_far, jax.tree.map(lambda part: part[k], everything))

    return lax.fori_loop(1, lax.axis_size(axis), lap, initial)


def send_rows(owner_ids, is_live, devices, slot_count):
    owner_hits = (
        (owner_ids[:, None] == jnp.arange(devices, dtype=jnp.int32)[None, :]) & is_live[:, None]
    ).astype(jnp.int32)
    rank_in = jnp.sum((jnp.cumsum(owner_hits, axis=0) - 1) * owner_hits, axis=1)
    return jnp.where(is_live, owner_ids * slot_count + rank_in, devices * slot_count)


def place_rows(arrays, row_index, length):
    return tuple(
        (
            jnp.zeros((length,) + source_rows.shape[1:], source_rows.dtype)
            .at[row_index]
            .set(source_rows, mode="drop")
            for source_rows in arrays
        )
    )


def keep_rows(recv_scales, devices, slot_count, own_max):
    is_used = recv_scales[:, 0] > 0
    counts = jnp.sum(is_used.reshape(devices, slot_count).astype(jnp.int32), axis=1)
    starts = jnp.repeat(
        jnp.cumsum(counts) - counts, slot_count, total_repeat_length=devices * slot_count
    )
    within = jnp.arange(devices * slot_count, dtype=jnp.int32) % slot_count
    return jnp.where(is_used, starts + within, own_max)


def attend(queried, key_rows, value_rows, key_scale, value_scale, is_live):
    page_count = key_rows.shape[0]
    key_f = (
        key_rows.reshape(page_count, PAGE, KEY_VALUE_HEADS, HEAD_SIZE).astype(jnp.float32)
        * key_scale.astype(jnp.float32)[:, None, :, None]
    ).reshape(page_count * PAGE, KEY_VALUE_HEADS, HEAD_SIZE)
    value_f = (
        value_rows.reshape(page_count, PAGE, KEY_VALUE_HEADS, HEAD_SIZE).astype(jnp.float32)
        * value_scale.astype(jnp.float32)[:, None, :, None]
    ).reshape(page_count * PAGE, KEY_VALUE_HEADS, HEAD_SIZE)
    scores = jnp.einsum(
        "bgrd,tgd->bgrt", queried, key_f, precision=lax.Precision.HIGHEST
    ) / math.sqrt(HEAD_SIZE)
    token_live = jnp.repeat(is_live, PAGE, total_repeat_length=page_count * PAGE)
    scores = jnp.where(token_live, scores, -1e30)
    maxima = jnp.max(scores, axis=-1)
    weights = jnp.where(token_live, jnp.exp(scores - maxima[..., None]), 0.0)
    mixture = jnp.einsum("bgrt,tgd->bgrd", weights, value_f, precision=lax.Precision.HIGHEST)
    return (maxima, jnp.sum(weights, axis=-1), mixture)


def combine(left_part, right_part):
    maxima = jnp.maximum(left_part[0], right_part[0])
    left_factor = jnp.exp(left_part[0] - maxima)
    right_factor = jnp.exp(right_part[0] - maxima)
    totals = left_part[1] * left_factor + right_part[1] * right_factor
    mixture = left_part[2] * left_factor[..., None] + right_part[2] * right_factor[..., None]
    return (maxima, totals, mixture)


def on_device(queries, kv_pages, page_scales, page_owner, valid_pages, branch_kv, parents):
    devices = lax.axis_size("seq")
    page_count = kv_pages.shape[0]
    slot_count = max(2, (page_count + devices - 1) // devices)
    own_max = slot_count * min(devices, page_count)
    group_size = HQ // KEY_VALUE_HEADS
    is_live = jnp.arange(page_count, dtype=jnp.int32) < valid_pages[0]
    outgoing = send_rows(page_owner, is_live, devices, slot_count)
    queried = queries.astype(jnp.float32).reshape(
        LAYERS, BEAMS, KEY_VALUE_HEADS, group_size, HEAD_SIZE
    )
    partials = []
    send_pages, send_scales = place_rows((kv_pages, page_scales), outgoing, devices * slot_count)
    recv_pages, recv_scales = (
        lax.all_to_all(send_pages, "seq", split_axis=0, concat_axis=0, tiled=True),
        lax.all_to_all(send_scales, "seq", split_axis=0, concat_axis=0, tiled=True),
    )
    page_cache, cache_scales = place_rows(
        (recv_pages, recv_scales), keep_rows(recv_scales, devices, slot_count, own_max), own_max
    )
    for current_layer_index in range(LAYERS):
        key_at = 2 * current_layer_index * KEY_VALUE_HEADS
        partials.append(
            attend(
                queried[current_layer_index],
                page_cache[:, 2 * current_layer_index],
                page_cache[:, 2 * current_layer_index + 1],
                cache_scales[:, key_at : key_at + KEY_VALUE_HEADS],
                cache_scales[:, key_at + KEY_VALUE_HEADS : key_at + 2 * KEY_VALUE_HEADS],
                cache_scales[:, key_at] > 0,
            )
        )
    maxima = jnp.stack([partial_value[0] for partial_value in partials])
    totals = jnp.stack([partial_value[1] for partial_value in partials])
    mixture = jnp.stack([partial_value[2] for partial_value in partials])
    maxima, totals, mixture = combined_all((maxima, totals, mixture), "seq", combine)
    chooser = (parents[:, None] == jnp.arange(BEAMS, dtype=jnp.int32)[None, :]).astype(jnp.float32)
    own_kv = jnp.einsum(
        "cp,lkpw->lkcw", chooser, branch_kv.astype(jnp.float32), precision=lax.Precision.HIGHEST
    )
    own_key = own_kv[:, 0].reshape(LAYERS, BEAMS, KEY_VALUE_HEADS, 1, HEAD_SIZE)
    own_value = own_kv[:, 1].reshape(LAYERS, BEAMS, KEY_VALUE_HEADS, 1, HEAD_SIZE)
    own_score = jnp.sum(queried * own_key, axis=-1) / math.sqrt(HEAD_SIZE)
    highest = jnp.maximum(maxima, own_score)
    merged_factor = jnp.exp(maxima - highest)
    own_factor = jnp.exp(own_score - highest)
    attended = (mixture * merged_factor[..., None] + own_factor[..., None] * own_value) / (
        totals * merged_factor + own_factor
    )[..., None]
    return (page_cache, cache_scales, attended.reshape(LAYERS, BEAMS, HQ * HEAD_SIZE))


def solution(mesh):
    return jax.shard_map(
        on_device,
        mesh=mesh,
        in_specs=(P(), P("seq", None, None, None), P("seq", None), P("seq"), P("seq"), P(), P()),
        out_specs=(P("seq", None, None, None), P("seq", None), P()),
        check_vma=False,
    )
```

profile of v0, /device:TPU:16, one launch (start us, length us, event | category | flops | bytes accessed | tf_op | source)
XLA Modules:
  0.0 448.9 jit_solution(16120939908111659084)
XLA Ops:
  13.6 5.9 %all-to-all-start = ((bf16[32,2,128]{2,1,0:T(2,128)(2,1)}), bf16[32,2,128]{2,1,0:T(2,128)(2,1)S(1)}, u32[]{:S(2)}, u32[]{:S(2)}) async-start(bf16[32,2,128]{2,1,0:T(2,128)(2,1)} %reshape.567), calls=%async_computation | async-start | bytes 32768 | tf_op jit(solution)/shard_map/all_to_all | solution.py:100
  19.5 6.3 %copy.78 = bf16[256,4,2,1024]{3,1,2,0:T(4,128)(2,1)} copy(bf16[256,4,2,1024]{3,2,1,0:T(2,128)(2,1)} %param.18) | data formatting | bytes 8388608 | tf_op args[1]
  25.8 4.1 broadcast.294.clone
  29.9 33.1 %scatter_fusion = bf16[256,4,2,1024]{3,1,2,0:T(4,128)(2,1)} fusion(bf16[256,4,2,1024]{3,1,2,0:T(4,128)(2,1)} %broadcast.294.clone, s32[256]{0:T(256)S(1)} %compare_select_fusion.4, bf16[256,4,2,1024]{3,1,2,0:T(4,128)(2,1)} %copy.78), kind=kCustom, calls=%fused_computation.3 | custom fusion | bytes 12583936 | tf_op jit(solution)/shard_map/scatter | solution.py:39
  63.1 6.2 %all-to-all-start.1 = ((bf16[256,4,2,1024]{3,1,2,0:T(4,128)(2,1)}), bf16[256,4,2,1024]{3,1,2,0:T(4,128)(2,1)}, u32[]{:S(2)}, u32[]{:S(2)}) async-start(bf16[256,4,2,1024]{3,1,2,0:T(4,128)(2,1)} %scatter_fusion), calls=%async_computation.1 | async-start | bytes 8388608 | tf_op jit(solution)/shard_map/all_to_all | solution.py:99
  70.1 2.3 scatter_custom_fusion.4
  75.3 4.5 select_reduce_fusion
  80.7 15.8 %select_select_fusion = s32[256]{0:T(256)S(1)} fusion(pred[256]{0:T(512)(128)(4,1)S(1)} %get-tuple-element.273, pred[256]{0:T(512)(128)(4,1)S(1)} %get-tuple-element.272, pred[256]{0:T(512)(128)(4,1)S(1)} %get-tuple-element.267, pred[256]{0:T(512)(128)(4,1)S(1)} %get-tuple-element.268, pred[256]{0:T(512)(128)(4,1)S(1)} %get-tuple-element.269, ...), kind=kLoop, calls=%fused_computation.143 | loop fusion | flops 6400 | bytes 8548 | tf_op jit(solution)/shard_map/jit(_take)/gather | solution.py:48
  98.7 3.4 gather_fusion
  102.1 3.4 gather_fusion.1
  106.0 53.9 %all-to-all-done.1 = bf16[256,4,2,1024]{3,1,2,0:T(4,128)(2,1)} async-done(((bf16[256,4,2,1024]{3,1,2,0:T(4,128)(2,1)}), bf16[256,4,2,1024]{3,1,2,0:T(4,128)(2,1)}, u32[]{:S(2)}, u32[]{:S(2)}) %all-to-all-start.1) | async-done | bytes 4194336 | tf_op jit(solution)/shard_map/all_to_all | solution.py:99
  160.0 4.0 broadcast.294
  164.0 33.2 %scatter_fusion.1 = bf16[256,4,2,1024]{3,1,2,0:T(4,128)(2,1)} fusion(bf16[256,4,2,1024]{3,1,2,0:T(4,128)(2,1)} %broadcast.294, s32[256]{0:T(256)S(1)} %fusion.50, bf16[256,4,2,1024]{3,1,2,0:T(4,128)(2,1)} %all-to-all-done.1), kind=kCustom, calls=%fused_computation.4 | custom fusion | bytes 12583936 | tf_op jit(solution)/shard_map/scatter | solution.py:39
  197.2 13.7 %slice_convert_fusion.1 = (f32[256,1,2,1024]{3,1,2,0:T(1,128)S(1)}, f32[256,1,2,1024]{3,1,2,0:T(1,128)S(1)}, f32[256,1,2,1024]{3,1,2,0:T(1,128)S(1)}, f32[256,1,2,1024]{3,1,2,0:T(1,128)S(1)}) fusion(bf16[256,4,2,1024]{3,1,2,0:T(4,128)(2,1)} %scatter_fusion.1), kind=kLoop, calls=%fused_computation.16 | loop fusion | flops 2097152 | bytes 12582912 | tf_op jit(solution)/shard_map/convert_element_type | solution.py:62
  210.9 1.7 fusion.81
  212.6 1.7 fusion.82
  214.4 1.9 fusion.32
  216.3 1.9 fusion.29
  220.4 8.5 %copy.102 = bf16[256,4,2,1024]{3,2,1,0:T(2,128)(2,1)} copy(bf16[256,4,2,1024]{3,1,2,0:T(4,128)(2,1)} %scatter_fusion.1) | data formatting | bytes 8388608
  228.9 53.0 %all-gather = f32[64,8,8,8]{3,2,1,0:T(8,128)S(1)} all-gather(f32[2,8,8,8]{3,2,1,0:T(8,128)S(1)} %copy.88), channel_id=2, replica_groups=mesh['seq'=32] {'seq'}, dimensions={0}, use_global_device_ids=true | all-gather | bytes 135168 | tf_op jit(solution)/shard_map/all_gather | solution.py:17
  284.0 60.1 %all-gather.1 = f32[64,8,8,8]{3,2,1,0:T(8,128)S(1)} all-gather(f32[2,8,8,8]{3,2,1,0:T(8,128)S(1)} %copy.89), channel_id=3, replica_groups=mesh['seq'=32] {'seq'}, dimensions={0}, use_global_device_ids=true | all-gather | bytes 135168 | tf_op jit(solution)/shard_map/all_gather | solution.py:17
  345.4 19.0 %all-gather.5.cloned.1.call-done = f32[64,8,8,8,128]{4,3,2,1,0:T(8,128)} async-done(((f32[2,8,8,8,128]{4,3,2,1,0:T(8,128)}), f32[64,8,8,8,128]{4,3,2,1,0:T(8,128)}) %all-gather.5.cloned.1.call-update) | async-done | bytes 16777232 | tf_op jit(solution)/shard_map/all_gather | solution.py:17
  365.5 74.7 %while.22 = (s32[]{:T(128)}, f32[2,8,8,8]{3,2,1,0:T(8,128)S(1)}, f32[2,8,8,8]{3,2,1,0:T(8,128)S(1)}, f32[2,8,8,8,128]{4,3,2,1,0:T(8,128)S(1)}, f32[32,2,8,8,8]{4...) while((s32[]{:T(128)}, f32[2,8,8,8]{3,2,1,0:T(8,128)S(1)}, ...), condition=%wide.region_17.19_spmd, body=%wide.region_16.18_spmd.sunk | while | flops 399365 | bytes 1613975 | solution.py:23
  380.9 1.4 fusion.87
  (157 shorter events, 93.8 us)
Async XLA Ops:
  7.2 212.0 %copy-start = (bf16[2,2,8,1024]{3,2,1,0:T(8,128)(2,1)S(1)}, bf16[2,2,8,1024]{3,2,1,0:T(8,128)(2,1)}, u32[]{:S(2)}) copy-start(bf16[2,2,8,1024]{3,2,1,0:T(8,128)(2,1)} %param.22) | copy-start | bytes 196612
  13.6 49.5 %all-to-all-start = ((bf16[32,2,128]{2,1,0:T(2,128)(2,1)}), bf16[32,2,128]{2,1,0:T(2,128)(2,1)S(1)}, u32[]{:S(2)}, u32[]{:S(2)}) async-start(bf16[32,2,128]{2,1,0:T(2,128)(2,1)} %reshape.567), calls=%async_computation | async-start | bytes 32768 | tf_op jit(solution)/shard_map/all_to_all | solution.py:100
  63.1 6.3 %copy-start.4 = (s32[2,128]{1,0:T(2,128)S(1)}, s32[2,128]{1,0:T(2,128)}, u32[]{:S(2)}) copy-start(s32[2,128]{1,0:T(2,128)} %constant.234.clone.1) | copy-start | bytes 3076
  63.1 6.7 %copy-start.5 = (s32[2,128]{1,0:T(2,128)S(1)}, s32[2,128]{1,0:T(2,128)}, u32[]{:S(2)}) copy-start(s32[2,128]{1,0:T(2,128)} %constant.239.clone.1) | copy-start | bytes 3076
  63.1 10.0 %copy-start.3 = (bf16[2,8,8192]{2,1,0:T(8,128)(2,1)S(1)}, bf16[2,8,8192]{2,1,0:T(8,128)(2,1)}, u32[]{:S(2)}) copy-start(bf16[2,8,8192]{2,1,0:T(8,128)(2,1)} %param.17) | copy-start | bytes 786436
  63.1 96.9 %all-to-all-start.1 = ((bf16[256,4,2,1024]{3,1,2,0:T(4,128)(2,1)}), bf16[256,4,2,1024]{3,1,2,0:T(4,128)(2,1)}, u32[]{:S(2)}, u32[]{:S(2)}) async-start(bf16[256,4,2,1024]{3,1,2,0:T(4,128)(2,1)} %scatter_fusion), calls=%async_computation.1 | async-start | bytes 8388608 | tf_op jit(solution)/shard_map/all_to_all | solution.py:99
  69.3 295.1 %all-gather.5.cloned.1.call-start = ((), (), s32[]{:S(2)}) async-start(), calls=%async_computation.2 | async-start | bytes 17301504 | tf_op jit(solution)/shard_map/all_gather | solution.py:17
  218.3 0.9 copy-start.6
  281.9 1.4 copy-start.1
  344.1 1.3 copy-start.2
Sparse Core Ops, SparseCore 0:
  219.3 145.0 all-gather.4
where the time goes:
time: 455 us; the launch traced here: 449 us
  other arithmetic  117 us (26%)
  blocking collectives  113 us (25%)
  local copies, waits for them, and re-layouts  110 us (24%)
  waiting for transfers between devices  72.9 us (16%)
  between operations  15.2 us (3%)
  starting transfers between devices  12.2 us (3%)
  matrix products  7.55 us (2%)
    all_gather x2, blocking collectives, combined_all(): everything = jax.tree.map(lambda part: lax.all_gather(part, axis), shard)  113 us
    scatter x4, local copies, waits for them, and re-layouts, place_rows(): return tuple((jnp.zeros((length,) + source_rows.shape[1:], source_rows.dt...  68.9 us
    all_to_all x1, waiting for transfers between devices, on_device(): lax.all_to_all(send_pages, 'seq', split_axis=0, concat_axis=0, tiled=True)  53.9 us
    add x31, other arithmetic, combine(): left_part[2] * left_factor[..., None]  44.7 us
    add x31, other arithmetic, combine(): totals = left_part[1] * left_factor + right_part[1] * right_factor  29.2 us
    gather x3, other arithmetic, keep_rows(): jnp.repeat(jnp.cumsum(counts) - counts, slot_count, total_repeat_length=d...  21.2 us
    unnamed x21, local copies, waits for them, and re-layouts  19.8 us
    all_gather x1, waiting for transfers between devices, combined_all(): everything = jax.tree.map(lambda part: lax.all_gather(part, axis), shard)  19 us
  transfers between devices with their start and end apart: 3, of which 2 were waited for; matrix products, arithmetic and copies ran while one was open for 20% of the time, Pallas kernels for 0%

commit v1 on v0

v1 whole, which is shorter than its diff:
```python
import math

import jax
import jax.numpy as jnp
from jax import lax
from jax.experimental import pallas as pl
from jax.experimental.pallas import tpu as pltpu
from jax.sharding import PartitionSpec as P

HQ = 64
KEY_VALUE_HEADS = 8
HEAD_SIZE = 128
LAYERS = 2
BEAMS = 8
PAGE = 2
WAIT_PAGES = 32


def wait_pages(count, like_ref, sem):
    size = min(WAIT_PAGES, like_ref.shape[0])
    many, few = like_ref.at[pl.ds(0, size)], like_ref.at[0]

    def many_at_once(_, carry):
        pltpu.make_async_copy(many, many, sem).wait()
        return carry

    def one(_, carry):
        pltpu.make_async_copy(few, few, sem).wait()
        return carry

    lax.fori_loop(0, count // size, many_at_once, 0)
    lax.fori_loop(0, count % size, one, 0)


def pack_kernel(slot_count, owner_s, valid_s, owner_v, scales_t, pages, send_pages, send_scales, taken, sem):
    page_count = pages.shape[0]
    devices = taken.shape[0]
    live_count = valid_s[0]

    def clear(d, carry):
        taken[d] = 0
        return carry

    lax.fori_loop(0, devices, clear, 0)

    def send(p, carry):
        owner = owner_s[p]
        rank = taken[owner]
        taken[owner] = rank + 1
        pltpu.make_async_copy(pages.at[p], send_pages.at[owner * slot_count + rank], sem).start()
        return carry

    lax.fori_loop(0, live_count, send, 0)
    owners = owner_v[...]
    page_row = lax.broadcasted_iota(jnp.int32, (page_count, page_count), 0)
    page_col = lax.broadcasted_iota(jnp.int32, (page_count, page_count), 1)
    owner_row = jnp.broadcast_to(owners, (page_count, page_count))
    owner_col = jnp.transpose(owner_row)
    earlier = jnp.where((owner_row == owner_col) & (page_row < page_col), 1, 0)
    rank = jnp.sum(earlier, axis=0, keepdims=True)
    slot = jnp.where(page_col[:1] < live_count, owners * slot_count + rank, -1)
    slot_row = lax.broadcasted_iota(jnp.int32, (devices * slot_count, page_count), 0)
    chosen = jnp.where(slot_row == slot, 1.0, 0.0).astype(jnp.bfloat16)
    send_scales[...] = lax.dot_general(
        chosen, scales_t[...], (((1,), (1,)), ((), ())), preferred_element_type=jnp.float32
    ).astype(jnp.bfloat16)
    wait_pages(live_count, send_pages, sem)


def unpack_kernel(used_s, used_v, recv_scales, recv_pages, page_cache, cache_scales_t, zero_page, sem):
    slots = recv_pages.shape[0]
    own_max = page_cache.shape[0]
    zero_page[...] = jnp.zeros_like(zero_page)

    def keep(slot, row):
        is_used = used_s[slot]

        @pl.when(is_used > 0)
        def _():
            pltpu.make_async_copy(recv_pages.at[slot], page_cache.at[row], sem).start()

        return row + is_used

    total = lax.fori_loop(0, slots, keep, 0)

    def blank(row, carry):
        pltpu.make_async_copy(zero_page.at[0], page_cache.at[row], sem).start()
        return carry

    lax.fori_loop(total, own_max, blank, 0)
    used = used_v[...]
    slot_row = lax.broadcasted_iota(jnp.int32, (slots, slots), 0)
    slot_col = lax.broadcasted_iota(jnp.int32, (slots, slots), 1)
    used_col = jnp.transpose(jnp.broadcast_to(used, (slots, slots)))
    row = jnp.sum(jnp.where(slot_row < slot_col, used_col, 0), axis=0, keepdims=True)
    row = jnp.where(used > 0, row, -1)
    row_id = lax.broadcasted_iota(jnp.int32, (own_max, slots), 0)
    chosen = jnp.where(row_id == row, 1.0, 0.0).astype(jnp.bfloat16)
    cache_scales_t[...] = lax.dot_general(
        recv_scales[...], chosen, (((0,), (1,)), ((), ())), preferred_element_type=jnp.float32
    ).astype(jnp.bfloat16)
    wait_pages(own_max, page_cache, sem)


def pack(kv_pages, page_scales, page_owner, valid_pages, devices, slot_count):
    page_count, scale_count = page_scales.shape
    any_spec = pl.BlockSpec(memory_space=pl.ANY)
    smem = pl.BlockSpec(memory_space=pltpu.SMEM)
    vmem = pl.BlockSpec(memory_space=pltpu.VMEM)
    return pl.pallas_call(
        lambda *refs: pack_kernel(slot_count, *refs),
        out_shape=(
            jax.ShapeDtypeStruct((devices * slot_count,) + kv_pages.shape[1:], kv_pages.dtype),
            jax.ShapeDtypeStruct((devices * slot_count, scale_count), page_scales.dtype),
        ),
        in_specs=[smem, smem, vmem, vmem, any_spec],
        out_specs=(any_spec, vmem),
        scratch_shapes=[pltpu.SMEM((devices,), jnp.int32), pltpu.SemaphoreType.DMA],
        name="pack",
    )(page_owner, valid_pages, page_owner.reshape(1, page_count), page_scales.T, kv_pages)


def unpack(recv_pages, recv_scales, own_max):
    slots, scale_count = recv_scales.shape
    any_spec = pl.BlockSpec(memory_space=pl.ANY)
    smem = pl.BlockSpec(memory_space=pltpu.SMEM)
    vmem = pl.BlockSpec(memory_space=pltpu.VMEM)
    used = (recv_scales[:, 0] > 0).astype(jnp.int32)
    page_cache, cache_scales_t = pl.pallas_call(
        unpack_kernel,
        out_shape=(
            jax.ShapeDtypeStruct((own_max,) + recv_pages.shape[1:], recv_pages.dtype),
            jax.ShapeDtypeStruct((scale_count, own_max), recv_scales.dtype),
        ),
        in_specs=[smem, vmem, vmem, any_spec],
        out_specs=(any_spec, vmem),
        scratch_shapes=[pltpu.VMEM((1,) + recv_pages.shape[1:], recv_pages.dtype), pltpu.SemaphoreType.DMA],
        name="unpack",
    )(used, used.reshape(1, slots), recv_scales, recv_pages)
    return page_cache, cache_scales_t.T


def attend(queried, key_rows, value_rows, key_scale, value_scale, token_live):
    token_count = key_rows.shape[0] * PAGE
    keys = key_rows.reshape(token_count, KEY_VALUE_HEADS, HEAD_SIZE)
    values = value_rows.reshape(token_count, KEY_VALUE_HEADS, HEAD_SIZE)
    pages = key_rows.shape[0]

    def by_token(scale):
        spread = jnp.broadcast_to(scale.T[:, :, None].astype(jnp.float32), (KEY_VALUE_HEADS, pages, PAGE))
        return spread.reshape(KEY_VALUE_HEADS, token_count)

    scores = jnp.einsum("bgrd,tgd->gbrt", queried, keys, preferred_element_type=jnp.float32)
    scores = scores * (by_token(key_scale) / math.sqrt(HEAD_SIZE))[:, None, None, :]
    scores = jnp.where(token_live, scores, -1e30)
    maxima = jnp.max(scores, axis=-1)
    weights = jnp.where(token_live, jnp.exp(scores - maxima[..., None]), 0.0)
    totals = jnp.sum(weights, axis=-1)
    scaled = weights * by_token(value_scale)[:, None, None, :]
    high = lax.reduce_precision(scaled, 8, 7)
    low = (scaled - high).astype(jnp.bfloat16)
    mix = lambda part: jnp.einsum("gbrt,tgd->gbrd", part, values, preferred_element_type=jnp.float32)
    mixture = mix(high.astype(jnp.bfloat16)) + mix(low)
    return (jnp.moveaxis(maxima, 0, 1), jnp.moveaxis(totals, 0, 1), jnp.moveaxis(mixture, 0, 1))


def on_device(queries, kv_pages, page_scales, page_owner, valid_pages, branch_kv, parents):
    devices = lax.axis_size("seq")
    page_count = kv_pages.shape[0]
    slot_count = max(2, (page_count + devices - 1) // devices)
    own_max = slot_count * min(devices, page_count)
    group_size = HQ // KEY_VALUE_HEADS
    send_pages, send_scales = pack(kv_pages, page_scales, page_owner, valid_pages, devices, slot_count)
    recv_pages = lax.all_to_all(send_pages, "seq", split_axis=0, concat_axis=0, tiled=True)
    recv_scales = lax.all_to_all(send_scales, "seq", split_axis=0, concat_axis=0, tiled=True)
    page_cache, cache_scales = unpack(recv_pages, recv_scales, own_max)

    token_live = jnp.arange(page_count * PAGE, dtype=jnp.int32) < valid_pages[0] * PAGE
    queried = queries.reshape(LAYERS, BEAMS, KEY_VALUE_HEADS, group_size, HEAD_SIZE)
    partials = []
    for layer in range(LAYERS):
        key_at = 2 * layer * KEY_VALUE_HEADS
        partials.append(
            attend(
                queried[layer],
                kv_pages[:, 2 * layer],
                kv_pages[:, 2 * layer + 1],
                page_scales[:, key_at : key_at + KEY_VALUE_HEADS],
                page_scales[:, key_at + KEY_VALUE_HEADS : key_at + 2 * KEY_VALUE_HEADS],
                token_live,
            )
        )
    rows = LAYERS * BEAMS * HQ
    row_share = rows // devices
    maxima, totals, mixture = (jnp.stack([part[i] for part in partials]) for i in range(3))
    outgoing = jnp.concatenate(
        [
            mixture.reshape(devices, row_share * HEAD_SIZE),
            maxima.reshape(devices, row_share),
            totals.reshape(devices, row_share),
        ],
        axis=1,
    )
    incoming = lax.all_to_all(outgoing, "seq", split_axis=0, concat_axis=0, tiled=True)
    mixture = incoming[:, : row_share * HEAD_SIZE].reshape(devices, row_share, HEAD_SIZE)
    maxima = incoming[:, row_share * HEAD_SIZE : row_share * (HEAD_SIZE + 1)]
    totals = incoming[:, row_share * (HEAD_SIZE + 1) :]

    own_at = branch_kv[:, :, parents].astype(jnp.float32)
    own_key = own_at[:, 0].reshape(LAYERS, BEAMS, KEY_VALUE_HEADS, 1, HEAD_SIZE)
    own_value = own_at[:, 1].reshape(LAYERS, BEAMS, KEY_VALUE_HEADS, 1, HEAD_SIZE)
    own_score = jnp.sum(queried.astype(jnp.float32) * own_key, axis=-1) / math.sqrt(HEAD_SIZE)
    own_value = jnp.broadcast_to(own_value, (LAYERS, BEAMS, KEY_VALUE_HEADS, group_size, HEAD_SIZE))
    me = lax.axis_index("seq")
    own_score = lax.dynamic_slice(own_score.reshape(rows), (me * row_share,), (row_share,))
    own_value = lax.dynamic_slice(own_value.reshape(rows, HEAD_SIZE), (me * row_share, 0), (row_share, HEAD_SIZE))
    highest = jnp.maximum(jnp.max(maxima, axis=0), own_score)
    factor = jnp.exp(maxima - highest)
    own_factor = jnp.exp(own_score - highest)
    total = jnp.sum(totals * factor, axis=0) + own_factor
    mixed = jnp.sum(mixture * factor[..., None], axis=0) + own_factor[:, None] * own_value
    share = mixed / total[:, None]
    attended = lax.all_gather(share, "seq", axis=0, tiled=True)
    return (page_cache, cache_scales, attended.reshape(LAYERS, BEAMS, HQ * HEAD_SIZE))


def solution(mesh):
    return jax.shard_map(
        on_device,
        mesh=mesh,
        in_specs=(P(), P("seq", None, None, None), P("seq", None), P("seq"), P("seq"), P(), P()),
        out_specs=(P("seq", None, None, None), P("seq", None), P()),
        check_vma=False,
    )
```

time: 455 us -> 435 us (0.956)
  Pallas kernels: 0 us -> 222 us
  other arithmetic: 117 us -> 3.56 us
  local copies, waits for them, and re-layouts: 110 us -> 20.6 us
  waiting for transfers between devices: 72.9 us -> 0.01 us
  starting transfers between devices: 12.2 us -> 35.3 us
  blocking collectives: 113 us -> 136 us
  between operations: 15.2 us -> 1.77 us
    pallas_call x0 -> x2, Pallas kernels: none -> 222 us  [the longest x1 117 us: unpack(): pl.pallas_call(unpack_kernel, out_shape=(jax.ShapeDtypeStruct((own_max,)...]
    add x63 -> x1, other arithmetic: 73.9 us -> 0.08 us  [on_device(): total = jnp.sum(totals * factor, axis=0) + own_factor]
    scatter x4 -> x0, local copies, waits for them, and re-layouts: 68.9 us -> none  [place_rows(): return tuple((jnp.zeros((length,) + source_rows.shape[1:], source_rows.dt...]
    all_to_all x1, waiting for transfers between devices: 53.9 us -> 0.01 us  [on_device(): lax.all_to_all(send_pages, 'seq', split_axis=0, concat_axis=0, tiled=True)]
    all_to_all x1, starting transfers between devices: 5.93 us -> 29.3 us  [on_device(): lax.all_to_all(send_scales, 'seq', split_axis=0, concat_axis=0, tiled=True)]
    gather x4 -> x1, other arithmetic: 21.2 us -> 0.01 us  [on_device(): own_at = branch_kv[:, :, parents].astype(jnp.float32)]
    all_to_all x0 -> x1, blocking collectives: none -> 19.2 us  [on_device(): lax.all_to_all(outgoing, 'seq', split_axis=0, concat_axis=0, tiled=True)]
    all_gather x1 -> x0, waiting for transfers between devices: 19 us -> none  [combined_all(): everything = jax.tree.map(lambda part: lax.all_gather(part, axis), shard)]
  transfers between devices with their start and end apart: 3 -> 2, of which waited for: 2 -> 0; matrix products, arithmetic and copies ran while one was open for 20% -> 7% of each run, Pallas kernels for 0% -> 0%
where the time goes in v1:
time: 435 us; the launch traced here: 426 us
  Pallas kernels  222 us (51%)
  blocking collectives  136 us (31%)
  starting transfers between devices  35.3 us (8%)
  local copies, waits for them, and re-layouts  20.6 us (5%)
  matrix products  7.56 us (2%)
    pallas_call x1, Pallas kernels, unpack(): pl.pallas_call(unpack_kernel, out_shape=(jax.ShapeDtypeStruct((own_max,)...  117 us
    all_gather x1, blocking collectives, on_device(): attended = lax.all_gather(share, 'seq', axis=0, tiled=True)  117 us
    pallas_call x1, Pallas kernels, pack(): pl.pallas_call(lambda *refs: pack_kernel(slot_count, *refs), out_shape=(j...  104 us
    all_to_all x1, starting transfers between devices, on_device(): lax.all_to_all(send_scales, 'seq', split_axis=0, concat_axis=0, tiled=True)  29.3 us
    all_to_all x1, blocking collectives, on_device(): lax.all_to_all(outgoing, 'seq', split_axis=0, concat_axis=0, tiled=True)  19.2 us
  transfers between devices with their start and end apart: 2, of which 0 were waited for; matrix products, arithmetic and copies ran while one was open for 7% of the time, Pallas kernels for 0%

profile of v1, /device:TPU:16, one launch (start us, length us, event | category | flops | bytes accessed | tf_op | source)
XLA Modules:
  0.0 426.2 jit_solution(14003401634076954841)
XLA Ops:
  1.3 104.4 %pack.1 = (bf16[256,4,2,1024]{3,2,1,0:T(2,128)(2,1)}, bf16[256,32]{1,0:T(8,128)(2,1)}) custom-call(s32[256]{0:T(256)} %refs_0_.1, s32[1]{0:T(128)S(6)} %copy.124.refs_1_, s32[1,256]{1,0:T(1,128)} %bitcast.113, bf16[32,256]{1,0:T(8,128)(2,1)} %bitcast.110, bf16[256,4,2,1024]{3,2,1,0:T(2,128)(2,1)} %refs_4_.1), custom_call_target="tpu_custom_call" | custom-call | tf_op jit(solution)/shard_map/pack/pallas_call | solution.py:110
  105.8 1.6 reshape.126
  107.3 29.3 %all-to-all-start = ((bf16[32,2,128]{2,1,0:T(2,128)(2,1)}), bf16[32,2,128]{2,1,0:T(2,128)(2,1)S(1)}, u32[]{:S(2)}, u32[]{:S(2)}) async-start(bf16[32,2,128]{2,1,0:T(2,128)(2,1)} %reshape.126), calls=%async_computation | async-start | bytes 32768 | tf_op jit(solution)/shard_map/all_to_all | solution.py:175
  136.7 5.5 %fusion.45 = (bf16[256,1,2,1024]{3,2,1,0:T(2,128)(2,1)}, bf16[256,1,2,1024]{3,2,1,0:T(2,128)(2,1)S(1)}, bf16[256,1,2,1024]{3,2,1,0:T(2,128)(2,1)}, bf16[256,1,2,1024]{3,2,1,0:T(2,128)(2,1)S(1)}) fusion(bf16[256,4,2,1024]{3,2,1,0:T(2,128)(2,1)} %refs_4_.1), kind=kLoop, calls=%fused_computation.82 | loop fusion | bytes 8388608 | tf_op jit(solution)/shard_map/slice | solution.py:186
  143.1 0.7 copy.56
  144.6 0.7 copy.64
  145.3 0.7 slice_bitcast_fusion.1
  146.0 1.7 reshape_squeeze.14
  147.8 1.5 reshape_squeeze.15
  149.3 1.8 copy_bitcast_fusion.1
  151.0 1.3 fusion.47
  152.3 1.8 fusion.12
  154.1 1.9 fusion.2
  156.0 1.5 reshape_squeeze.17
  157.5 0.7 reshape_squeeze.16
  158.2 1.6 fusion.46
  159.8 1.3 fusion.14
  163.3 19.2 %all_to_all.28 = f32[32,1,4160]{2,1,0:T(1,128)S(1)} all-to-all(f32[32,1,4160]{2,1,0:T(1,128)S(1)} %copy.70), channel_id=1, replica_groups=mesh['seq'=32] {'seq'}, dimensions={0} | all-to-all | bytes 1064960 | tf_op jit(solution)/shard_map/all_to_all | solution.py:204
  182.5 6.0 %all-to-all-start.1 = ((bf16[256,4,2,1024]{3,2,1,0:T(2,128)(2,1)}), bf16[256,4,2,1024]{3,2,1,0:T(2,128)(2,1)}, u32[]{:S(2)}, u32[]{:S(2)}) async-start(bf16[256,4,2,1024]{3,2,1,0:T(2,128)(2,1)} %get-tuple-element.8), calls=%async_computation.1 | async-start | bytes 8388608 | tf_op jit(solution)/shard_map/all_to_all | solution.py:174
  188.5 0.7 gather_fusion
  189.8 0.7 convert_reduce_fusion.used_s
  191.5 116.7 %all_gather.3 = f32[1024,128]{1,0:T(8,128)S(1)} all-gather(f32[32,128]{1,0:T(8,128)S(1)} %fusion.39), channel_id=1, replica_groups=mesh['seq'=32] {'seq'}, dimensions={0}, use_global_device_ids=true | all-gather | bytes 540672 | tf_op jit(solution)/shard_map/all_gather | solution.py:223
  308.1 0.9 reshape.105
  309.0 117.2 %unpack.1 = (bf16[256,4,2,1024]{3,2,1,0:T(2,128)(2,1)}, bf16[32,256]{1,0:T(8,128)(2,1)}) custom-call(s32[256]{0:T(256)} %convert_reduce_fusion.used_s, s32[1,256]{1,0:T(1,128)} %bitcast.112, bf16[256,32]{1,0:T(8,128)(2,1)} %bitcast.104, bf16[256,4,2,1024]{3,2,1,0:T(2,128)(2,1)} %all-to-all-done.1.recv_pages), custom_call_target="tpu_custom_call" | custom-call | tf_op jit(solution)/shard_map/unpack/pallas_call | solution.py:129
  (69 shorter events, 5.2 us)
Async XLA Ops:
  0.6 187.8 %copy-start = (bf16[2,2,8,1024]{3,2,1,0:T(8,128)(2,1)S(1)}, bf16[2,2,8,1024]{3,2,1,0:T(8,128)(2,1)}, u32[]{:S(2)}) copy-start(bf16[2,2,8,1024]{3,2,1,0:T(8,128)(2,1)} %param.12) | copy-start | bytes 196612
  0.6 136.0 %copy-start.7 = (bf16[256,32]{0,1:T(8,128)(2,1)S(1)}, bf16[256,32]{0,1:T(8,128)(2,1)}, u32[]{:S(2)}) copy-start(bf16[256,32]{0,1:T(8,128)(2,1)} %param.9) | copy-start | bytes 49156
  107.3 55.9 %all-to-all-start = ((bf16[32,2,128]{2,1,0:T(2,128)(2,1)}), bf16[32,2,128]{2,1,0:T(2,128)(2,1)S(1)}, u32[]{:S(2)}, u32[]{:S(2)}) async-start(bf16[32,2,128]{2,1,0:T(2,128)(2,1)} %reshape.126), calls=%async_computation | async-start | bytes 32768 | tf_op jit(solution)/shard_map/all_to_all | solution.py:175
  136.7 8.6 %copy-start.4 = (bf16[2,8,8192]{2,1,0:T(8,128)(2,1)S(1)}, bf16[2,8,8192]{2,1,0:T(8,128)(2,1)}, u32[]{:S(2)}) copy-start(bf16[2,8,8192]{2,1,0:T(8,128)(2,1)} %param.7) | copy-start | bytes 786436
  149.3 4.8 %copy-start.3 = (bf16[512,8,128]{2,1,0:T(8,128)(2,1)S(1)}, bf16[512,8,128]{2,1,0:T(8,128)(2,1)}, u32[]{:S(2)}) copy-start(bf16[512,8,128]{2,1,0:T(8,128)(2,1)} %reshape_squeeze.15) | copy-start | bytes 3145732
  152.3 3.8 copy-start.1
  156.0 5.1 %copy-start.8 = (f32[8,512]{1,0:T(8,128)S(1)}, f32[8,512]{1,0:T(8,128)}, u32[]{:S(2)}) copy-start(f32[8,512]{1,0:T(8,128)} %copy.64) | copy-start | bytes 49156
  158.2 2.9 copy-start.2
  158.2 2.9 copy-start.9
  159.8 2.4 copy-start.6
  182.5 6.0 %copy-start.10 = (s32[8]{0:T(128)S(1)}, s32[8]{0:T(128)}, u32[]{:S(2)}) copy-start(s32[8]{0:T(128)} %param.13) | copy-start | bytes 100
  182.5 126.6 %all-to-all-start.1 = ((bf16[256,4,2,1024]{3,2,1,0:T(2,128)(2,1)}), bf16[256,4,2,1024]{3,2,1,0:T(2,128)(2,1)}, u32[]{:S(2)}, u32[]{:S(2)}) async-start(bf16[256,4,2,1024]{3,2,1,0:T(2,128)(2,1)} %get-tuple-element.8), calls=%async_computation.1 | async-start | bytes 8388608 | tf_op jit(solution)/shard_map/all_to_all | solution.py:174
  189.8 119.2 %copy-start.5 = (bf16[32,8,32]{2,1,0:T(8,128)(2,1)}, bf16[32,8,32]{2,1,0:T(8,128)(2,1)S(1)}, u32[]{:S(2)}) copy-start(bf16[32,8,32]{2,1,0:T(8,128)(2,1)S(1)} %reshape.127) | copy-start | bytes 49156

commit v2 on v1

--- a/solution.py
+++ b/solution.py
@@ -6,6 +6,7 @@
 from jax.experimental import pallas as pl
 from jax.experimental.pallas import tpu as pltpu
 from jax.sharding import PartitionSpec as P
+
 
 HQ = 64
 KEY_VALUE_HEADS = 8
@@ -14,6 +15,7 @@
 BEAMS = 8
 PAGE = 2
 WAIT_PAGES = 32
+FETCH_CHUNKS = 4
 
 
 def wait_pages(count, like_ref, sem):
@@ -32,10 +34,19 @@
     lax.fori_loop(0, count % size, one, 0)
 
 
-def pack_kernel(slot_count, owner_s, valid_s, owner_v, scales_t, pages, send_pages, send_scales, taken, sem):
+def pack_kernel(slot_count, owner_s, valid_s, owner_v, scales_t, pages, send_pages, send_scales, held, taken, sem, in_sems):
     page_count = pages.shape[0]
     devices = taken.shape[0]
     live_count = valid_s[0]
+    chunks = in_sems.shape[0]
+    size = page_count // chunks
+
+    def fetch(c):
+        part = pl.ds(c * size, size)
+        return pltpu.make_async_copy(pages.at[part], held.at[part], in_sems.at[c])
+
+    for c in range(chunks):
+        fetch(c).start()
 
     def clear(d, carry):
         taken[d] = 0
@@ -47,10 +58,12 @@
         owner = owner_s[p]
         rank = taken[owner]
         taken[owner] = rank + 1
-        pltpu.make_async_copy(pages.at[p], send_pages.at[owner * slot_count + rank], sem).start()
-        return carry
-
-    lax.fori_loop(0, live_count, send, 0)
+        pltpu.make_async_copy(held.at[p], send_pages.at[owner * slot_count + rank], sem).start()
+        return carry
+
+    for c in range(chunks):
+        fetch(c).wait()
+        lax.fori_loop(c * size, jnp.clip(live_count, c * size, (c + 1) * size), send, 0)
     owners = owner_v[...]
     page_row = lax.broadcasted_iota(jnp.int32, (page_count, page_count), 0)
     page_col = lax.broadcasted_iota(jnp.int32, (page_count, page_count), 1)
@@ -67,9 +80,18 @@
     wait_pages(live_count, send_pages, sem)
 
 
-def unpack_kernel(used_s, used_v, recv_scales, recv_pages, page_cache, cache_scales_t, zero_page, sem):
+def unpack_kernel(used_s, used_v, recv_scales, recv_pages, page_cache, cache_scales_t, held, zero_page, sem, in_sems):
     slots = recv_pages.shape[0]
     own_max = page_cache.shape[0]
+    chunks = in_sems.shape[0]
+    size = slots // chunks
+
+    def fetch(c):
+        part = pl.ds(c * size, size)
+        return pltpu.make_async_copy(recv_pages.at[part], held.at[part], in_sems.at[c])
+
+    for c in range(chunks):
+        fetch(c).start()
     zero_page[...] = jnp.zeros_like(zero_page)
 
     def keep(slot, row):
@@ -77,11 +99,14 @@
 
         @pl.when(is_used > 0)
         def _():
-            pltpu.make_async_copy(recv_pages.at[slot], page_cache.at[row], sem).start()
+            pltpu.make_async_copy(held.at[slot], page_cache.at[row], sem).start()
 
         return row + is_used
 
-    total = lax.fori_loop(0, slots, keep, 0)
+    total = 0
+    for c in range(chunks):
+        fetch(c).wait()
+        total = lax.fori_loop(c * size, (c + 1) * size, keep, total)
 
     def blank(row, carry):
         pltpu.make_async_copy(zero_page.at[0], page_cache.at[row], sem).start()
@@ -102,6 +127,10 @@
     wait_pages(own_max, page_cache, sem)
 
 
+def fetch_chunks(pages):
+    return math.gcd(FETCH_CHUNKS, pages)
+
+
 def pack(kv_pages, page_scales, page_owner, valid_pages, devices, slot_count):
     page_count, scale_count = page_scales.shape
     any_spec = pl.BlockSpec(memory_space=pl.ANY)
@@ -115,7 +144,12 @@
         ),
         in_specs=[smem, smem, vmem, vmem, any_spec],
         out_specs=(any_spec, vmem),
-        scratch_shapes=[pltpu.SMEM((devices,), jnp.int32), pltpu.SemaphoreType.DMA],
+        scratch_shapes=[
+            pltpu.VMEM(kv_pages.shape, kv_pages.dtype),
+            pltpu.SMEM((devices,), jnp.int32),
+            pltpu.SemaphoreType.DMA,
+            pltpu.SemaphoreType.DMA((fetch_chunks(page_count),)),
+        ],
         name="pack",
     )(page_owner, valid_pages, page_owner.reshape(1, page_count), page_scales.T, kv_pages)
 
@@ -134,7 +168,12 @@
         ),
         in_specs=[smem, vmem, vmem, any_spec],
         out_specs=(any_spec, vmem),
-        scratch_shapes=[pltpu.VMEM((1,) + recv_pages.shape[1:], recv_pages.dtype), pltpu.SemaphoreType.DMA],
+        scratch_shapes=[
+            pltpu.VMEM(recv_pages.shape, recv_pages.dtype),
+            pltpu.VMEM((1,) + recv_pages.shape[1:], recv_pages.dtype),
+            pltpu.SemaphoreType.DMA,
+            pltpu.SemaphoreType.DMA((fetch_chunks(slots),)),
+        ],
         name="unpack",
     )(used, used.reshape(1, slots), recv_scales, recv_pages)
     return page_cache, cache_scales_t.T
@@ -164,6 +203,53 @@
     return (jnp.moveaxis(maxima, 0, 1), jnp.moveaxis(totals, 0, 1), jnp.moveaxis(mixture, 0, 1))
 
 
+def bits_of(devices):
+    masks, mask = [], 1
+    while mask < devices:
+        masks.append(mask)
+        mask *= 2
+    return masks
+
+
+def swap(array, mask, devices):
+    return lax.ppermute(array, "seq", [(i, i ^ mask) for i in range(devices)])
+
+
+def as_rows(values):
+    count = -(-values.shape[0] // HEAD_SIZE)
+    return jnp.pad(values, (0, count * HEAD_SIZE - values.shape[0])).reshape(count, HEAD_SIZE)
+
+
+def reduce_step(state, blocks, axis, mask, is_high, devices):
+    maxima, totals, mixture = state
+    half = maxima.shape[0] // 2
+    low, high = [part[:half] for part in state], [part[half:] for part in state]
+    kept = [jnp.where(is_high, h, l) for l, h in zip(low, high)]
+    sent = [jnp.where(is_high, l, h) for l, h in zip(low, high)]
+    low_block, high_block = (lax.index_in_dim(blocks, i, axis, keepdims=False) for i in range(2))
+    kept_block = jnp.where(is_high, high_block, low_block)
+    sent_block = jnp.where(is_high, low_block, high_block)
+    small = as_rows(jnp.concatenate([sent[0], sent[1]]))
+    block_rows = sent_block.reshape(-1, HEAD_SIZE)
+    received = swap(jnp.concatenate([sent[2], block_rows, small]), mask, devices)
+    got_small = received[half + block_rows.shape[0] :].reshape(-1)
+    got_block = received[half : half + block_rows.shape[0]].reshape(sent_block.shape)
+    got_maxima, got_totals = got_small[:half], got_small[half : 2 * half]
+    highest = jnp.maximum(kept[0], got_maxima)
+    factor, got_factor = jnp.exp(kept[0] - highest), jnp.exp(got_maxima - highest)
+    totals = kept[1] * factor + got_totals * got_factor
+    mixture = kept[2] * factor[:, None] + received[:half] * got_factor[:, None]
+    blocks = jnp.where(
+        is_high, jnp.stack([got_block, kept_block], axis), jnp.stack([kept_block, got_block], axis)
+    )
+    return (highest, totals, mixture), blocks
+
+
+def gather_step(rows, mask, is_high, devices):
+    received = swap(rows, mask, devices)
+    return jnp.where(is_high, jnp.concatenate([received, rows]), jnp.concatenate([rows, received]))
+
+
 def on_device(queries, kv_pages, page_scales, page_owner, valid_pages, branch_kv, parents):
     devices = lax.axis_size("seq")
     page_count = kv_pages.shape[0]
@@ -172,8 +258,6 @@
     group_size = HQ // KEY_VALUE_HEADS
     send_pages, send_scales = pack(kv_pages, page_scales, page_owner, valid_pages, devices, slot_count)
     recv_pages = lax.all_to_all(send_pages, "seq", split_axis=0, concat_axis=0, tiled=True)
-    recv_scales = lax.all_to_all(send_scales, "seq", split_axis=0, concat_axis=0, tiled=True)
-    page_cache, cache_scales = unpack(recv_pages, recv_scales, own_max)
 
     token_live = jnp.arange(page_count * PAGE, dtype=jnp.int32) < valid_pages[0] * PAGE
     queried = queries.reshape(LAYERS, BEAMS, KEY_VALUE_HEADS, group_size, HEAD_SIZE)
@@ -191,36 +275,36 @@
             )
         )
     rows = LAYERS * BEAMS * HQ
-    row_share = rows // devices
     maxima, totals, mixture = (jnp.stack([part[i] for part in partials]) for i in range(3))
-    outgoing = jnp.concatenate(
-        [
-            mixture.reshape(devices, row_share * HEAD_SIZE),
-            maxima.reshape(devices, row_share),
-            totals.reshape(devices, row_share),
-        ],
-        axis=1,
-    )
-    incoming = lax.all_to_all(outgoing, "seq", split_axis=0, concat_axis=0, tiled=True)
-    mixture = incoming[:, : row_share * HEAD_SIZE].reshape(devices, row_share, HEAD_SIZE)
-    maxima = incoming[:, row_share * HEAD_SIZE : row_share * (HEAD_SIZE + 1)]
-    totals = incoming[:, row_share * (HEAD_SIZE + 1) :]
+    state = (maxima.reshape(rows), totals.reshape(rows), mixture.reshape(rows, HEAD_SIZE))
+    me = lax.axis_index("seq")
+    masks = bits_of(devices)
+    block_size = slot_count * page_scales.shape[1]
+    blocks = send_scales.astype(jnp.float32).reshape((2,) * len(masks) + (block_size,))
+    for at, mask in enumerate(masks):
+        state, blocks = reduce_step(state, blocks, len(masks) - 1 - at, mask, (me & mask) != 0, devices)
+    recv_scales = blocks.reshape(devices * slot_count, page_scales.shape[1]).astype(page_scales.dtype)
 
     own_at = branch_kv[:, :, parents].astype(jnp.float32)
     own_key = own_at[:, 0].reshape(LAYERS, BEAMS, KEY_VALUE_HEADS, 1, HEAD_SIZE)
     own_value = own_at[:, 1].reshape(LAYERS, BEAMS, KEY_VALUE_HEADS, 1, HEAD_SIZE)
     own_score = jnp.sum(queried.astype(jnp.float32) * own_key, axis=-1) / math.sqrt(HEAD_SIZE)
     own_value = jnp.broadcast_to(own_value, (LAYERS, BEAMS, KEY_VALUE_HEADS, group_size, HEAD_SIZE))
-    me = lax.axis_index("seq")
-    own_score = lax.dynamic_slice(own_score.reshape(rows), (me * row_share,), (row_share,))
-    own_value = lax.dynamic_slice(own_value.reshape(rows, HEAD_SIZE), (me * row_share, 0), (row_share, HEAD_SIZE))
-    highest = jnp.maximum(jnp.max(maxima, axis=0), own_score)
+    row_share = rows // devices
+    order = sum(jnp.where((me & mask) != 0, devices // (2 * mask), 0) for mask in masks)
+    first = order * row_share
+    own_score = lax.dynamic_slice(own_score.reshape(rows), (first,), (row_share,))
+    own_value = lax.dynamic_slice(own_value.reshape(rows, HEAD_SIZE), (first, 0), (row_share, HEAD_SIZE))
+    maxima, totals, mixture = state
+    highest = jnp.maximum(maxima, own_score)
     factor = jnp.exp(maxima - highest)
     own_factor = jnp.exp(own_score - highest)
-    total = jnp.sum(totals * factor, axis=0) + own_factor
-    mixed = jnp.sum(mixture * factor[..., None], axis=0) + own_factor[:, None] * own_value
-    share = mixed / total[:, None]
-    attended = lax.all_gather(share, "seq", axis=0, tiled=True)
+    total = totals * factor + own_factor
+    share = (mixture * factor[:, None] + own_factor[:, None] * own_value) / total[:, None]
+    attended = share
+    for mask in reversed(masks):
+        attended = gather_step(attended, mask, (me & mask) != 0, devices)
+    page_cache, cache_scales = unpack(recv_pages, recv_scales, own_max)
     return (page_cache, cache_scales, attended.reshape(LAYERS, BEAMS, HQ * HEAD_SIZE))
 
 

time: 435 us -> 171 us (0.39)
  the two profiles are of different devices: /device:TPU:16 before, /device:TPU:0 now
where the time goes in v2:
time: 171 us
  waiting for transfers between devices  102 us (60%)
  local copies, waits for them, and re-layouts  27.2 us (16%)
  starting transfers between devices  16.6 us (10%)
  Pallas kernels  9.98 us (6%)
  matrix products  7.69 us (4%)
  other arithmetic  5.28 us (3%)
  between operations  1.94 us (1%)
    ppermute x10, waiting for transfers between devices, swap(): return lax.ppermute(array, 'seq', [(i, i ^ mask) for i in range(devices)])  102 us
    ppermute x10, starting transfers between devices, swap(): return lax.ppermute(array, 'seq', [(i, i ^ mask) for i in range(devices)])  9.77 us
    all_to_all x1, starting transfers between devices, on_device(): lax.all_to_all(send_pages, 'seq', split_axis=0, concat_axis=0, tiled=True)  6.8 us
    slice x1, local copies, waits for them, and re-layouts, on_device(): kv_pages[:, 2 * layer + 1]  5.46 us
    pallas_call x1, Pallas kernels, unpack(): pl.pallas_call(unpack_kernel, out_shape=(jax.ShapeDtypeStruct((own_max,)...  5.25 us
    broadcast_in_dim x4, local copies, waits for them, and re-layouts, by_token(): jnp.broadcast_to(scale.T[:, :, None].astype(jnp.float32), (KEY_VALUE_HEAD...  5.18 us
    pallas_call x1, Pallas kernels, pack(): pl.pallas_call(lambda *refs: pack_kernel(slot_count, *refs), out_shape=(j...  4.73 us
    dot_general x4, matrix products, attend(): jnp.einsum('gbrt,tgd->gbrd', part, values, preferred_element_type=jnp.flo...  4.58 us
  transfers between devices with their start and end apart: 11, of which 9 were waited for; matrix products, arithmetic and copies ran while one was open for 3% of the time, Pallas kernels for 0%

profile of v2, /device:TPU:0, one launch (start us, length us, event | category | flops | bytes accessed | tf_op | source)
XLA Modules:
  0.0 170.6 jit_solution(2076652196637417684)
XLA Ops:
  3.3 5.5 %fusion.77 = (bf16[256,1,2,1024]{3,2,1,0:T(2,128)(2,1)S(1)}, bf16[256,1,2,1024]{3,2,1,0:T(2,128)(2,1)}, bf16[256,1,2,1024]{3,2,1,0:T(2,128)(2,1)}, bf16[256,1,2,1024]{3,2,1,0:T(2,128)(2,1)S(1)}) fusion(bf16[256,4,2,1024]{3,2,1,0:T(2,128)(2,1)} %refs_4_.1), kind=kLoop, calls=%fused_computation.181 | loop fusion | bytes 8388608 | tf_op jit(solution)/shard_map/slice | solution.py:271
  8.8 1.7 %reshape_squeeze.16 = bf16[512,8,128]{2,1,0:T(8,128)(2,1)S(1)} reshape(bf16[256,1,2,1024]{3,2,1,0:T(2,128)(2,1)} %get-tuple-element.35) | data formatting | bytes 2097152 | tf_op jit(solution)/shard_map/reshape;squeeze | solution.py:184
  11.3 1.7 broadcast_in_dim.35
  16.6 1.6 fusion.79
  18.2 1.7 fusion.7
  19.9 1.9 %convolution_add_fusion = f32[8,8,8,128]{3,2,1,0:T(8,128)} fusion(f32[8,8,8,128]{3,2,1,0:T(8,128)S(1)} %fusion.7, bf16[512,8,128,1]{2,1,0,3:T(8,128)(2,1)S(1)} %bitcast.155, f32[8,8,8,512]{3,2,1,0:T(8,128)S(1)} %get-tuple-element.65, f32[8,512]{1,0:T(8,128)S(1)} %copy.94, f32[8,8,8]{2,1,0:T(8,128)S(1)} %get-tuple-element.64, pred[512]{0:T(512)(128)(4,1)} %iota_compare_fusion), kind=kOutput, calls=%fused_computation.9 | convolution fusion | flops 68747264 | bytes 2640384 | tf_op jit(solution)/shard_map/gbrt,tgd->gbrd/dot_general | solution.py:201
  21.7 1.7 %reshape_squeeze.14 = bf16[512,8,128]{2,1,0:T(8,128)(2,1)S(1)} reshape(bf16[256,1,2,1024]{3,2,1,0:T(2,128)(2,1)} %get-tuple-element.36) | data formatting | bytes 2097152 | tf_op jit(solution)/shard_map/reshape;squeeze | solution.py:184
  24.3 1.7 broadcast_in_dim.31
  27.0 1.5 reshape_squeeze.15
  29.3 1.7 broadcast_in_dim.34
  32.0 1.5 fusion.78
  35.5 4.7 %pack.1 = (bf16[256,4,2,1024]{3,2,1,0:T(2,128)(2,1)}, bf16[256,32]{1,0:T(8,128)(2,1)}) custom-call(s32[256]{0:T(256)} %refs_0_.1, s32[1]{0:T(128)S(6)} %copy.167.refs_1_, s32[1,256]{1,0:T(1,128)} %bitcast.170, bf16[32,256]{1,0:T(8,128)(2,1)} %bitcast.163, bf16[256,4,2,1024]{3,2,1,0:T(2,128)(2,1)} %refs_4_.1), custom_call_target="tpu_custom_call" | custom-call | tf_op jit(solution)/shard_map/pack/pallas_call | solution.py:139
  42.4 6.8 %all-to-all-start = ((bf16[256,4,2,1024]{3,2,1,0:T(2,128)(2,1)}), bf16[256,4,2,1024]{3,2,1,0:T(2,128)(2,1)}, u32[]{:S(2)}, u32[]{:S(2)}) async-start(bf16[256,4,2,1024]{3,2,1,0:T(2,128)(2,1)} %get-tuple-element.8), calls=%async_computation | async-start | bytes 8388608 | tf_op jit(solution)/shard_map/all_to_all | solution.py:260
  50.9 1.8 %collective-permute-start.1 = (f32[292,128]{1,0:T(8,128)S(1)}, f32[292,128]{1,0:T(8,128)S(1)}, u32[]{:S(2)}, u32[]{:S(2)}) collective-permute-start(f32[292,128]{1,0:T(8,128)S(1)} %pad_maximum_fusion.1), channel_id=1, source_target_pairs={{0,2},{1,3},{2,0},{3,1},{4,6},{5,7},{6,4},{7,5},{8,10},{9,11},{10,... | collective-permute-start | bytes 448520 | tf_op jit(solution)/shard_map/ppermute | solution.py:215
  52.6 28.8 %collective-permute-done.1 = f32[292,128]{1,0:T(8,128)S(1)} collective-permute-done((f32[292,128]{1,0:T(8,128)S(1)}, f32[292,128]{1,0:T(8,128)S(1)}, u32[]{:S(2)}, u32[]{:S(2)}) %collective-permute-start.1) | collective-permute-done | bytes 149536 | tf_op jit(solution)/shard_map/ppermute | solution.py:215
  81.9 4.9 %collective-permute-done.2 = f32[162,128]{1,0:T(8,128)S(1)} collective-permute-done((f32[162,128]{1,0:T(8,128)S(1)}, f32[162,128]{1,0:T(8,128)S(1)}, u32[]{:S(2)}, u32[]{:S(2)}) %collective-permute-start.2) | collective-permute-done | bytes 82976 | tf_op jit(solution)/shard_map/ppermute | solution.py:215
  87.6 31.9 %collective-permute-done.3 = f32[97,128]{1,0:T(8,128)S(1)} collective-permute-done((f32[97,128]{1,0:T(8,128)S(1)}, f32[97,128]{1,0:T(8,128)S(1)}, u32[]{:S(2)}, u32[]{:S(2)}) %collective-permute-start.3) | collective-permute-done | bytes 49696 | tf_op jit(solution)/shard_map/ppermute | solution.py:215
  120.0 3.9 %collective-permute-start.4 = (f32[65,128]{1,0:T(8,128)S(1)}, f32[65,128]{1,0:T(8,128)S(1)}, u32[]{:S(2)}, u32[]{:S(2)}) collective-permute-start(f32[65,128]{1,0:T(8,128)S(1)} %pad_maximum_fusion.4), channel_id=1, source_target_pairs={{0,16},{1,17},{2,18},{3,19},{4,20},{5,21},{6,22},{7,23},{8,24},{9,... | collective-permute-start | bytes 99848 | tf_op jit(solution)/shard_map/ppermute | solution.py:215
  124.1 20.4 %collective-permute-done.4 = f32[65,128]{1,0:T(8,128)S(1)} collective-permute-done((f32[65,128]{1,0:T(8,128)S(1)}, f32[65,128]{1,0:T(8,128)S(1)}, u32[]{:S(2)}, u32[]{:S(2)}) %collective-permute-start.4) | collective-permute-done | bytes 33312 | tf_op jit(solution)/shard_map/ppermute | solution.py:215
  144.8 4.6 %collective-permute-done.5 = f32[32,128]{1,0:T(8,128)S(1)} collective-permute-done((f32[32,128]{1,0:T(8,128)S(1)}, f32[32,128]{1,0:T(8,128)S(1)}, u32[]{:S(2)}, u32[]{:S(2)}) %collective-permute-start.5) | collective-permute-done | bytes 16416 | tf_op jit(solution)/shard_map/ppermute | solution.py:215
  149.4 3.9 %collective-permute-done.6 = f32[64,128]{1,0:T(8,128)S(1)} collective-permute-done((f32[64,128]{1,0:T(8,128)S(1)}, f32[64,128]{1,0:T(8,128)S(1)}, u32[]{:S(2)}, u32[]{:S(2)}) %collective-permute-start.6) | collective-permute-done | bytes 32800 | tf_op jit(solution)/shard_map/ppermute | solution.py:215
  154.7 3.0 %collective-permute-done.7 = f32[128,128]{1,0:T(8,128)S(1)} collective-permute-done((f32[128,128]{1,0:T(8,128)S(1)}, f32[128,128]{1,0:T(8,128)S(1)}, u32[]{:S(2)}, u32[]{:S(2)}) %collective-permute-start.7) | collective-permute-done | bytes 65568 | tf_op jit(solution)/shard_map/ppermute | solution.py:215
  159.1 3.7 %collective-permute-done.8 = f32[256,128]{1,0:T(8,128)S(1)} collective-permute-done((f32[256,128]{1,0:T(8,128)S(1)}, f32[256,128]{1,0:T(8,128)S(1)}, u32[]{:S(2)}, u32[]{:S(2)}) %collective-permute-start.8) | collective-permute-done | bytes 131104 | tf_op jit(solution)/shard_map/ppermute | solution.py:215
  165.3 5.3 %unpack.1 = (bf16[256,4,2,1024]{3,2,1,0:T(2,128)(2,1)}, bf16[32,256]{1,0:T(8,128)(2,1)}) custom-call(s32[256]{0:T(256)} %convert_reduce_fusion.used_s, s32[1,256]{1,0:T(1,128)} %bitcast.169, bf16[256,32]{1,0:T(8,128)(2,1)} %copy-done.4, bf16[256,4,2,1024]{3,2,1,0:T(2,128)(2,1)} %all-to-all-done.recv_pages), custom_call_target="tpu_custom_call" | custom-call | tf_op jit(solution)/shard_map/unpack/pallas_call | solution.py:163
  (132 shorter events, 22.7 us)
Async XLA Ops:
  0.6 49.0 %copy-start = (bf16[2,2,8,1024]{3,2,1,0:T(8,128)(2,1)S(1)}, bf16[2,2,8,1024]{3,2,1,0:T(8,128)(2,1)}, u32[]{:S(2)}) copy-start(bf16[2,2,8,1024]{3,2,1,0:T(8,128)(2,1)} %param.12) | copy-start | bytes 196612
  3.3 10.7 %copy-start.3 = (bf16[2,8,8192]{2,1,0:T(8,128)(2,1)S(1)}, bf16[2,8,8192]{2,1,0:T(8,128)(2,1)}, u32[]{:S(2)}) copy-start(bf16[2,8,8192]{2,1,0:T(8,128)(2,1)} %param.7) | copy-start | bytes 786436
  16.6 3.3 %copy-start.2 = (bf16[512,8,128]{2,1,0:T(8,128)(2,1)S(1)}, bf16[512,8,128]{2,1,0:T(8,128)(2,1)}, u32[]{:S(2)}) copy-start(bf16[512,8,128]{2,1,0:T(8,128)(2,1)} %reshape_squeeze.17) | copy-start | bytes 3145732
  21.7 10.3 %copy-start.5 = (pred[512]{0:T(512)(128)(4,1)S(1)}, pred[512]{0:T(512)(128)(4,1)}, u32[]{:S(2)}) copy-start(pred[512]{0:T(512)(128)(4,1)} %iota_compare_fusion) | copy-start | bytes 1540
  28.5 5.7 %copy-start.1 = (bf16[512,8,128]{2,1,0:T(8,128)(2,1)S(1)}, bf16[512,8,128]{2,1,0:T(8,128)(2,1)}, u32[]{:S(2)}) copy-start(bf16[512,8,128]{2,1,0:T(8,128)(2,1)} %reshape_squeeze.15) | copy-start | bytes 3145732
  32.0 2.7 %copy-start.7 = (f32[8,8,8,128]{3,2,1,0:T(8,128)S(1)}, f32[8,8,8,128]{3,2,1,0:T(8,128)}, u32[]{:S(2)}) copy-start(f32[8,8,8,128]{3,2,1,0:T(8,128)} %convolution_add_fusion) | copy-start | bytes 786436
  41.3 9.1 %collective-permute-start = (f32[552,128]{1,0:T(8,128)S(1)}, f32[552,128]{1,0:T(8,128)S(1)}, u32[]{:S(2)}, u32[]{:S(2)}) collective-permute-start(f32[552,128]{1,0:T(8,128)S(1)} %pad_maximum_fusion), channel_id=1, source_target_pairs={{0,1},{1,0},{2,3},{3,2},{4,5},{5,4},{6,7},{7,6},{8,9},{9,8},{10,11... | collective-permute-start | bytes 847880 | tf_op jit(solution)/shard_map/ppermute | solution.py:215
  42.4 7.2 %copy-start.6 = (s32[8]{0:T(128)S(1)}, s32[8]{0:T(128)}, u32[]{:S(2)}) copy-start(s32[8]{0:T(128)} %param.13) | copy-start | bytes 100
  42.4 122.9 %all-to-all-start = ((bf16[256,4,2,1024]{3,2,1,0:T(2,128)(2,1)}), bf16[256,4,2,1024]{3,2,1,0:T(2,128)(2,1)}, u32[]{:S(2)}, u32[]{:S(2)}) async-start(bf16[256,4,2,1024]{3,2,1,0:T(2,128)(2,1)} %get-tuple-element.8), calls=%async_computation | async-start | bytes 8388608 | tf_op jit(solution)/shard_map/all_to_all | solution.py:260
  50.9 30.6 %collective-permute-start.1 = (f32[292,128]{1,0:T(8,128)S(1)}, f32[292,128]{1,0:T(8,128)S(1)}, u32[]{:S(2)}, u32[]{:S(2)}) collective-permute-start(f32[292,128]{1,0:T(8,128)S(1)} %pad_maximum_fusion.1), channel_id=1, source_target_pairs={{0,2},{1,3},{2,0},{3,1},{4,6},{5,7},{6,4},{7,5},{8,10},{9,11},{10,... | collective-permute-start | bytes 448520 | tf_op jit(solution)/shard_map/ppermute | solution.py:215
  81.8 5.1 %collective-permute-start.2 = (f32[162,128]{1,0:T(8,128)S(1)}, f32[162,128]{1,0:T(8,128)S(1)}, u32[]{:S(2)}, u32[]{:S(2)}) collective-permute-start(f32[162,128]{1,0:T(8,128)S(1)} %pad_maximum_fusion.2), channel_id=1, source_target_pairs={{0,4},{1,5},{2,6},{3,7},{4,0},{5,1},{6,2},{7,3},{8,12},{9,13},{10,... | collective-permute-start | bytes 248840 | tf_op jit(solution)/shard_map/ppermute | solution.py:215
  87.3 32.2 %collective-permute-start.3 = (f32[97,128]{1,0:T(8,128)S(1)}, f32[97,128]{1,0:T(8,128)S(1)}, u32[]{:S(2)}, u32[]{:S(2)}) collective-permute-start(f32[97,128]{1,0:T(8,128)S(1)} %pad_maximum_fusion.3), channel_id=1, source_target_pairs={{0,8},{1,9},{2,10},{3,11},{4,12},{5,13},{6,14},{7,15},{8,0},{9,1},... | collective-permute-start | bytes 149000 | tf_op jit(solution)/shard_map/ppermute | solution.py:215
  120.0 24.5 %collective-permute-start.4 = (f32[65,128]{1,0:T(8,128)S(1)}, f32[65,128]{1,0:T(8,128)S(1)}, u32[]{:S(2)}, u32[]{:S(2)}) collective-permute-start(f32[65,128]{1,0:T(8,128)S(1)} %pad_maximum_fusion.4), channel_id=1, source_target_pairs={{0,16},{1,17},{2,18},{3,19},{4,20},{5,21},{6,22},{7,23},{8,24},{9,... | collective-permute-start | bytes 99848 | tf_op jit(solution)/shard_map/ppermute | solution.py:215
  144.7 4.7 %collective-permute-start.5 = (f32[32,128]{1,0:T(8,128)S(1)}, f32[32,128]{1,0:T(8,128)S(1)}, u32[]{:S(2)}, u32[]{:S(2)}) collective-permute-start(f32[32,128]{1,0:T(8,128)S(1)} %fusion.43), channel_id=1, source_target_pairs={{0,16},{1,17},{2,18},{3,19},{4,20},{5,21},{6,22},{7,23},{8,24},{9,... | collective-permute-start | bytes 49160 | tf_op jit(solution)/shard_map/ppermute | solution.py:215
  149.4 3.9 %collective-permute-start.6 = (f32[64,128]{1,0:T(8,128)S(1)}, f32[64,128]{1,0:T(8,128)S(1)}, u32[]{:S(2)}, u32[]{:S(2)}) collective-permute-start(f32[64,128]{1,0:T(8,128)S(1)} %maximum_select_fusion.9), channel_id=1, source_target_pairs={{0,8},{1,9},{2,10},{3,11},{4,12},{5,13},{6,14},{7,15},{8,0},{9,1},... | collective-permute-start | bytes 98312 | tf_op jit(solution)/shard_map/ppermute | solution.py:215
  153.4 4.3 %collective-permute-start.7 = (f32[128,128]{1,0:T(8,128)S(1)}, f32[128,128]{1,0:T(8,128)S(1)}, u32[]{:S(2)}, u32[]{:S(2)}) collective-permute-start(f32[128,128]{1,0:T(8,128)S(1)} %maximum_select_fusion.3), channel_id=1, source_target_pairs={{0,4},{1,5},{2,6},{3,7},{4,0},{5,1},{6,2},{7,3},{8,12},{9,13},{10,... | collective-permute-start | bytes 196616 | tf_op jit(solution)/shard_map/ppermute | solution.py:215
  157.7 5.0 %collective-permute-start.8 = (f32[256,128]{1,0:T(8,128)S(1)}, f32[256,128]{1,0:T(8,128)S(1)}, u32[]{:S(2)}, u32[]{:S(2)}) collective-permute-start(f32[256,128]{1,0:T(8,128)S(1)} %maximum_select_fusion.2), channel_id=1, source_target_pairs={{0,2},{1,3},{2,0},{3,1},{4,6},{5,7},{6,4},{7,5},{8,10},{9,11},{10,... | collective-permute-start | bytes 393224 | tf_op jit(solution)/shard_map/ppermute | solution.py:215
  162.8 1.6 collective-permute-start.9
  163.0 2.3 %copy-start.4 = (bf16[256,32]{1,0:T(8,128)(2,1)}, bf16[256,32]{1,0:T(8,128)(2,1)S(1)}, u32[]{:S(2)}) copy-start(bf16[256,32]{1,0:T(8,128)(2,1)S(1)} %convert_element_type.73.recv_scales) | copy-start | bytes 49156

commit v3 on v0

v3 whole, which is shorter than its diff:
```python
import math

import jax
import jax.numpy as jnp
from jax import lax
from jax.experimental import pallas as pl
from jax.experimental.pallas import tpu as pltpu
from jax.sharding import PartitionSpec as P


HQ = 64
KEY_VALUE_HEADS = 8
HEAD_SIZE = 128
LAYERS = 2
BEAMS = 8
PAGE = 2
WAIT_PAGES = 32
MIB = 1 << 20
ISSUE = 8
CHUNKS = 4
FIRST_PART = 0.75


def wait_pages(count, like_ref, sem):
    size = min(WAIT_PAGES, like_ref.shape[0])
    many, few = like_ref.at[pl.ds(0, size)], like_ref.at[0]

    def many_at_once(_, carry):
        pltpu.make_async_copy(many, many, sem).wait()
        return carry

    def one(_, carry):
        pltpu.make_async_copy(few, few, sem).wait()
        return carry

    lax.fori_loop(0, count // size, many_at_once, 0)
    lax.fori_loop(0, count % size, one, 0)


def owner_ranks(owner_v):
    page_count = owner_v.shape[1]
    page_row = lax.broadcasted_iota(jnp.int32, (page_count, page_count), 0)
    page_col = lax.broadcasted_iota(jnp.int32, (page_count, page_count), 1)
    owner_row = jnp.broadcast_to(owner_v[...], (page_count, page_count))
    owner_col = jnp.transpose(owner_row)
    earlier = jnp.where((owner_row == owner_col) & (page_col < page_row), 1, 0)
    return owner_col[:, :1], jnp.sum(earlier, axis=1, keepdims=True)


def pack_pages(first_rank, slots, live_count, owner_v, pages, send, held, pages_v, pages_s, sem, in_sems, out_sem):
    page_count = pages.shape[0]
    total = send.shape[0]
    owner, rank = owner_ranks(owner_v)
    page_id = lax.broadcasted_iota(jnp.int32, (page_count, 1), 0)
    chosen = (page_id < live_count) & (rank >= first_rank) & (rank < first_rank + slots)
    place = jnp.where(chosen, owner * slots + rank - first_rank, -1)
    slot_id = lax.broadcasted_iota(jnp.int32, (page_count, total), 1)
    pages_v[...] = jnp.sum(jnp.where(place == slot_id, page_id, 0), axis=0, keepdims=True)
    to_scalars = pltpu.make_async_copy(pages_v, pages_s, sem)
    to_scalars.start()
    to_scalars.wait()
    chunks = in_sems.shape[0]
    size = total // chunks
    issue = math.gcd(size, ISSUE)
    for c in range(chunks):

        def fetch(step, carry):
            for i in range(issue):
                slot = c * size + step * issue + i
                pltpu.make_async_copy(pages.at[pages_s[0, slot]], held.at[slot], in_sems.at[c]).start()
            return carry

        lax.fori_loop(0, size // issue, fetch, 0)
    outs = []
    for c in range(chunks):
        part = pl.ds(c * size, size)
        pltpu.make_async_copy(held.at[part], held.at[part], in_sems.at[c]).wait()
        outs.append(pltpu.make_async_copy(held.at[part], send.at[part], out_sem.at[c]))
        outs[-1].start()
    for copy in outs:
        copy.wait()


def pack_first_kernel(slots, valid_s, owner_v, pages, send, *scratch):
    pack_pages(0, slots, valid_s[0], owner_v, pages, send, *scratch)


def pack_rest_kernel(first_slots, slot_count, valid_s, owner_v, scales_t, pages, send, send_scales, *scratch):
    page_count = pages.shape[0]
    slots = send_scales.shape[0]
    owner, rank = owner_ranks(owner_v)
    page_id = lax.broadcasted_iota(jnp.int32, (page_count, 1), 0)
    place = jnp.where(page_id < valid_s[0], owner * slot_count + rank, -1)
    slot_id = lax.broadcasted_iota(jnp.int32, (page_count, slots), 1)
    chosen = jnp.where(place == slot_id, 1.0, 0.0).astype(jnp.bfloat16)
    send_scales[...] = lax.dot_general(
        chosen, scales_t[...], (((0,), (1,)), ((), ())), preferred_element_type=jnp.float32
    )
    pack_pages(first_slots, slot_count - first_slots, valid_s[0], owner_v, pages, send, *scratch)


def unpack_first_kernel(counts_s, used_v, recv_scales, recv_pages, page_cache, cache_scales_t, zero_page, sem):
    own_max = page_cache.shape[0]
    slots = recv_scales.shape[0]
    devices = counts_s.shape[0]
    first_slots = recv_pages.shape[0] // devices
    zero_page[...] = jnp.zeros_like(zero_page)

    def keep(source, carry):
        row, copied = carry
        count = counts_s[source]

        def one(slot, inner):
            pltpu.make_async_copy(recv_pages.at[source * first_slots + slot], page_cache.at[row + slot], sem).start()
            return inner

        here = jnp.minimum(count, first_slots)
        lax.fori_loop(0, here, one, 0)
        return row + count, copied + here

    total, copied = lax.fori_loop(0, devices, keep, (0, 0))

    def blank(row, inner):
        pltpu.make_async_copy(zero_page.at[0], page_cache.at[row], sem).start()
        return inner

    lax.fori_loop(total, own_max, blank, 0)
    used = used_v[...]
    slot_row = lax.broadcasted_iota(jnp.int32, (slots, slots), 0)
    slot_col = lax.broadcasted_iota(jnp.int32, (slots, slots), 1)
    used_col = jnp.transpose(jnp.broadcast_to(used, (slots, slots)))
    row = jnp.sum(jnp.where(slot_row < slot_col, used_col, 0), axis=0, keepdims=True)
    row = jnp.where(used > 0, row, -1)
    row_id = lax.broadcasted_iota(jnp.int32, (own_max, slots), 0)
    chosen = jnp.where(row_id == row, 1.0, 0.0).astype(jnp.bfloat16)
    cache_scales_t[...] = lax.dot_general(
        recv_scales[...], chosen, (((0,), (1,)), ((), ())), preferred_element_type=jnp.float32
    ).astype(jnp.bfloat16)
    wait_pages(copied + own_max - total, page_cache, sem)


def unpack_rest_kernel(first_slots, counts_s, recv_pages, _, page_cache, held, sem, in_sems):
    devices = counts_s.shape[0]
    rest_slots = recv_pages.shape[0] // devices
    chunks = in_sems.shape[0]
    size = recv_pages.shape[0] // chunks
    parts = [pl.ds(c * size, size) for c in range(chunks)]
    fetches = [pltpu.make_async_copy(recv_pages.at[part], held.at[part], in_sems.at[c]) for c, part in enumerate(parts)]
    for fetch in fetches:
        fetch.start()

    def keep(source, carry):
        row, copied = carry
        count = counts_s[source]

        def one(slot, inner):
            pltpu.make_async_copy(
                held.at[source * rest_slots + slot], page_cache.at[row + first_slots + slot], sem
            ).start()
            return inner

        here = jnp.maximum(count - first_slots, 0)
        lax.fori_loop(0, here, one, 0)
        return row + count, copied + here

    carry = (0, 0)
    for c, fetch in enumerate(fetches):
        fetch.wait()
        carry = lax.fori_loop(c * size // rest_slots, (c + 1) * size // rest_slots, keep, carry)
    wait_pages(carry[1], page_cache, sem)


ANY = pl.BlockSpec(memory_space=pl.ANY)
SMEM = pl.BlockSpec(memory_space=pltpu.SMEM)
VMEM = pl.BlockSpec(memory_space=pltpu.VMEM)


def in_hbm(array):
    return pltpu.with_memory_space_constraint(array, pltpu.HBM)


def in_vmem(array):
    return pltpu.with_memory_space_constraint(array, pltpu.VMEM)


def pack_scratch(kv_pages, slots, chunks):
    return [
        pltpu.VMEM((slots,) + kv_pages.shape[1:], kv_pages.dtype),
        pltpu.VMEM((1, slots), jnp.int32),
        pltpu.SMEM((1, slots), jnp.int32),
        pltpu.SemaphoreType.DMA,
        pltpu.SemaphoreType.DMA((chunks,)),
        pltpu.SemaphoreType.DMA((chunks,)),
    ]


def pack_first(kv_pages, page_owner, valid_pages, devices, slots):
    page_count = kv_pages.shape[0]
    return pl.pallas_call(
        lambda *refs: pack_first_kernel(slots, *refs),
        out_shape=pltpu.HBM((devices * slots,) + kv_pages.shape[1:], kv_pages.dtype),
        in_specs=[SMEM, VMEM, ANY],
        out_specs=ANY,
        scratch_shapes=pack_scratch(kv_pages, devices * slots, math.gcd(CHUNKS, devices)),
        compiler_params=pltpu.CompilerParams(vmem_limit_bytes=8 * MIB),
        name="pack_first",
    )(valid_pages, page_owner.reshape(1, page_count), in_hbm(kv_pages))


def pack_rest(kv_pages, page_scales, page_owner, valid_pages, devices, slot_count, first_slots):
    page_count, scale_count = page_scales.shape
    slots = devices * (slot_count - first_slots)
    return pl.pallas_call(
        lambda *refs: pack_rest_kernel(first_slots, slot_count, *refs),
        out_shape=(
            pltpu.HBM((slots,) + kv_pages.shape[1:], kv_pages.dtype),
            pltpu.VMEM((devices * slot_count, scale_count), jnp.float32),
        ),
        in_specs=[SMEM, VMEM, VMEM, ANY],
        out_specs=(ANY, VMEM),
        scratch_shapes=pack_scratch(kv_pages, slots, math.gcd(CHUNKS, devices)),
        compiler_params=pltpu.CompilerParams(vmem_limit_bytes=8 * MIB),
        name="pack_rest",
    )(valid_pages, page_owner.reshape(1, page_count), page_scales.T, in_hbm(kv_pages))


def unpack_first(recv_pages, recv_scales, counts, own_max):
    slots, scale_count = recv_scales.shape
    used = (recv_scales[:, 0] > 0).astype(jnp.int32)
    return pl.pallas_call(
        lambda *refs: unpack_first_kernel(*refs),
        out_shape=(
            jax.ShapeDtypeStruct((own_max,) + recv_pages.shape[1:], recv_pages.dtype),
            jax.ShapeDtypeStruct((scale_count, own_max), recv_scales.dtype),
        ),
        in_specs=[SMEM, VMEM, VMEM, VMEM],
        out_specs=(ANY, VMEM),
        scratch_shapes=[
            pltpu.VMEM((1,) + recv_pages.shape[1:], recv_pages.dtype),
            pltpu.SemaphoreType.DMA,
        ],
        compiler_params=pltpu.CompilerParams(vmem_limit_bytes=4 * MIB),
        name="unpack_first",
    )(counts, used.reshape(1, slots), recv_scales, in_vmem(recv_pages))


def unpack_rest(recv_pages, counts, page_cache, first_slots):
    devices = counts.shape[0]
    return pl.pallas_call(
        lambda *refs: unpack_rest_kernel(first_slots, *refs),
        out_shape=jax.ShapeDtypeStruct(page_cache.shape, page_cache.dtype),
        in_specs=[SMEM, ANY, ANY],
        out_specs=ANY,
        input_output_aliases={2: 0},
        scratch_shapes=[
            pltpu.VMEM(recv_pages.shape, recv_pages.dtype),
            pltpu.SemaphoreType.DMA,
            pltpu.SemaphoreType.DMA((math.gcd(CHUNKS, devices),)),
        ],
        compiler_params=pltpu.CompilerParams(vmem_limit_bytes=4 * MIB),
        name="unpack_rest",
    )(counts, in_hbm(recv_pages), page_cache)


def as_row(column):
    return jnp.transpose(jnp.broadcast_to(column, (column.shape[0], HEAD_SIZE)))[:1]


def spread_rows(row):
    return jnp.transpose(jnp.broadcast_to(row, (HEAD_SIZE, row.shape[1])))


def small_count(share):
    return -(-2 * share // HEAD_SIZE)


def put_small(out, share, maxima, totals):
    both = jnp.concatenate([maxima, totals], axis=1)
    for at in range(small_count(share)):
        part = both[:, at * HEAD_SIZE : (at + 1) * HEAD_SIZE]
        out[share + at : share + at + 1, : part.shape[1]] = part


def get_small(rows, share):
    both = jnp.concatenate([rows[at : at + 1] for at in range(small_count(share))], axis=1)
    return both[:, :share], both[:, share : 2 * share]


def attend_kernel(units, place_s, valid_s, queries, scales_t, blocks, pages, *rest):
    outs, (token_scales, held, sems) = rest[:-3], rest[-3:]
    page_count = pages.shape[0]
    tokens = page_count * PAGE
    unit_rows = queries.shape[2]
    share = units * unit_rows
    groups, _, block_rows, _ = blocks.shape
    near = place_s[0]

    def unit_at(step, u):
        unit = (near ^ step) * units + u
        return unit // KEY_VALUE_HEADS, unit % KEY_VALUE_HEADS

    def fetch(step, u):
        layer, head = unit_at(step, u)
        lanes = pl.ds(pl.multiple_of(head * HEAD_SIZE, HEAD_SIZE), HEAD_SIZE)
        at = step * units + u
        return pltpu.make_async_copy(pages.at[:, pl.ds(2 * layer, 2), :, lanes], held.at[at], sems.at[at])

    order = [(step, u) for step in range(len(outs)) for u in range(units)]
    for step, u in order:
        fetch(step, u).start()
    page_id = lax.broadcasted_iota(jnp.int32, (page_count, tokens), 0)
    token_id = lax.broadcasted_iota(jnp.int32, (page_count, tokens), 1)
    spread = jnp.where(token_id // PAGE == page_id, 1.0, 0.0).astype(jnp.bfloat16)
    token_scales[...] = jnp.dot(scales_t[...], spread, preferred_element_type=jnp.float32)
    token_live = lax.broadcasted_iota(jnp.int32, (unit_rows, tokens), 1) < valid_s[0] * PAGE
    for step, out in enumerate(outs):
        maxima, totals = [], []
        for u in range(units):
            layer, head = unit_at(step, u)
            fetch(step, u).wait()
            keys = held[step * units + u, :, 0].reshape(tokens, HEAD_SIZE)
            values = held[step * units + u, :, 1].reshape(tokens, HEAD_SIZE)
            key_at = 2 * layer * KEY_VALUE_HEADS + head
            key_scale = token_scales[pl.ds(key_at, 1)] * (1 / math.sqrt(HEAD_SIZE))
            value_scale = token_scales[pl.ds(key_at + KEY_VALUE_HEADS, 1)]
            scores = lax.dot_general(
                queries[layer, head], keys, (((1,), (1,)), ((), ())), preferred_element_type=jnp.float32
            )
            scores = jnp.where(token_live, scores * key_scale, -1e30)
            highest = jnp.max(scores, axis=1, keepdims=True)
            weights = jnp.where(token_live, jnp.exp(scores - highest), 0.0)
            maxima.append(highest)
            totals.append(jnp.sum(weights, axis=1, keepdims=True))
            scaled = weights * value_scale
            high = scaled.astype(jnp.bfloat16)
            low = (scaled - high.astype(jnp.float32)).astype(jnp.bfloat16)
            mix = lambda part: jnp.dot(part, values, preferred_element_type=jnp.float32)
            out[u * unit_rows : (u + 1) * unit_rows] = mix(high) + mix(low)
        put_small(out, share, as_row(jnp.concatenate(maxima)), as_row(jnp.concatenate(totals)))
        for group in range(groups):
            at = share + small_count(share) + group * block_rows
            out[at : at + block_rows] = blocks[group, near ^ step]


def put_state(out, share, highest, total, mixture):
    out[:share] = mixture
    put_small(out, share, highest, total)


def put_blocks(payload, kept, first, entries, entry_at, size):
    for index in range(entries):
        payload[first + index * size : first + (index + 1) * size] = entry_at(0, index)
        kept[index * size : (index + 1) * size] = entry_at(1, index)


def merge_near_kernel(share, block_rows, groups, place_s, *refs):
    pieces, (payload, kept, sources) = refs[:-3], refs[-3:]
    near, far = place_s[0], place_s[1]
    first = share + small_count(share)
    smalls = [get_small(piece[share:first], share) for piece in pieces]
    highest = smalls[0][0]
    for maxima, _ in smalls[1:]:
        highest = jnp.maximum(highest, maxima)
    total, mixture = 0.0, 0.0
    for piece, (maxima, totals) in zip(pieces, smalls):
        factor = jnp.exp(maxima - highest)
        total += totals * factor
        mixture += piece[:share] * spread_rows(factor)
    put_state(payload, share, highest, total, mixture)
    for group in range(groups):
        for at, piece in enumerate(pieces):
            source = first + group * block_rows
            sources[group, pl.ds((near ^ at) * block_rows, block_rows)] = piece[source : source + block_rows]
    bit = far & 1

    def entry_at(mine, index):
        return sources[2 * index + (bit if mine else 1 - bit)]

    put_blocks(payload, kept, first, groups // 2, entry_at, sources.shape[1])


def far_merge(step, share, entry, place_s, own, kept, got, blocks):
    bit = (place_s[1] >> step) & 1
    first = share + small_count(share)
    entries = kept.shape[0] // entry
    width = 1 << step
    for index in range(entries):
        target, source = index // width, index % width
        at = target * 2 * width + source
        blocks[at + bit * width] = kept[index * entry : (index + 1) * entry]
        blocks[at + (1 - bit) * width] = got[first + index * entry : first + (index + 1) * entry]
    parts = []
    for rows, rows_other in ((own, got), (got, own)):
        pick = lambda at: jnp.where(bit == 0, rows[at], rows_other[at])
        maxima, totals = get_small(pick(slice(share, first)), share)
        parts.append((maxima, totals, pick(slice(0, share))))
    return parts


def merge_mid_kernel(step, share, entry, place_s, own, kept, got, payload, next_kept, blocks):
    (low_max, low_total, low_mix), (high_max, high_total, high_mix) = far_merge(
        step, share, entry, place_s, own, kept, got, blocks
    )
    highest = jnp.maximum(low_max, high_max)
    low, high = jnp.exp(low_max - highest), jnp.exp(high_max - highest)
    put_state(
        payload,
        share,
        highest,
        low_total * low + high_total * high,
        low_mix * spread_rows(low) + high_mix * spread_rows(high),
    )
    bit = (place_s[1] >> (step + 1)) & 1
    width = 2 << step

    def entry_at(mine, index):
        target, source = index // width, index % width
        return blocks[(2 * target + (bit if mine else 1 - bit)) * width + source]

    put_blocks(payload, next_kept, share + small_count(share), blocks.shape[0] // 2, entry_at, entry)


def merge_far_kernel(units, step, entry, place_s, parents_s, queries, branch, own, kept, got, out, out_blocks, blocks):
    near = place_s[0]
    unit_rows = queries.shape[2]
    share = units * unit_rows
    group_size = unit_rows // BEAMS
    states = far_merge(step, share, entry, place_s, own, kept, got, blocks)
    for index in range(blocks.shape[0]):
        out_blocks[index * entry : (index + 1) * entry] = blocks[index]
    beam_id = lax.broadcasted_iota(jnp.int32, (BEAMS, HEAD_SIZE), 0)
    own_scores, own_values = [], []
    for u in range(units):
        unit = near * units + u
        layer, head = unit // KEY_VALUE_HEADS, unit % KEY_VALUE_HEADS
        lanes = pl.ds(pl.multiple_of(head * HEAD_SIZE, HEAD_SIZE), HEAD_SIZE)
        keys, values = (branch[layer, kind, :, lanes].astype(jnp.float32) for kind in range(2))

        def chosen(rows):
            picked = [
                jnp.sum(jnp.where(beam_id == parents_s[beam], rows, 0.0), axis=0, keepdims=True)
                for beam in range(BEAMS)
            ]
            return jnp.concatenate([jnp.broadcast_to(row, (group_size, HEAD_SIZE)) for row in picked])

        own_scores.append(
            jnp.sum(queries[layer, head].astype(jnp.float32) * chosen(keys), axis=1, keepdims=True)
        )
        own_values.append(chosen(values))
    own_score = as_row(jnp.concatenate(own_scores)) / math.sqrt(HEAD_SIZE)
    highest = own_score
    for maxima, _, _ in states:
        highest = jnp.maximum(highest, maxima)
    factors = [jnp.exp(maxima - highest) for maxima, _, _ in states]
    own_factor = jnp.exp(own_score - highest)
    total = own_factor
    for (_, totals, _), factor in zip(states, factors):
        total += totals * factor
    mixture = jnp.concatenate(own_values) * spread_rows(own_factor / total)
    for (_, _, part), factor in zip(states, factors):
        mixture += part * spread_rows(factor / total)
    out[...] = mixture


def assemble_kernel(units, place_s, *refs):
    pieces, out = refs[:-1], refs[-1]
    unit_rows = pieces[0].shape[0] // units
    group_size = unit_rows // BEAMS
    for step, piece in enumerate(pieces):
        for u in range(units):
            unit = (place_s[0] ^ step) * units + u
            layer, head = unit // KEY_VALUE_HEADS, unit % KEY_VALUE_HEADS
            for query in range(group_size):
                at = pl.multiple_of((head * group_size + query) * HEAD_SIZE, HEAD_SIZE)
                out[layer, :, pl.ds(at, HEAD_SIZE)] = piece[pl.ds(u * unit_rows + query, BEAMS, stride=group_size)]


def partial_of(rows):
    return pltpu.VMEM((rows, HEAD_SIZE), jnp.float32)


def attend(place, queried, kv_pages, page_scales, valid_pages, blocks):
    page_count, scale_count = page_scales.shape
    groups, inner, block_rows, _ = blocks.shape
    units = LAYERS * KEY_VALUE_HEADS // inner
    share = units * queried.shape[2]
    return pl.pallas_call(
        lambda *refs: attend_kernel(units, *refs),
        in_specs=[SMEM, SMEM, VMEM, VMEM, VMEM, ANY],
        out_specs=(VMEM,) * inner,
        out_shape=(partial_of(share + small_count(share) + groups * block_rows),) * inner,
        scratch_shapes=[
            pltpu.VMEM((scale_count, page_count * PAGE), jnp.float32),
            pltpu.VMEM((inner * units, page_count, 2, PAGE, HEAD_SIZE), kv_pages.dtype),
            pltpu.SemaphoreType.DMA((inner * units,)),
        ],
        compiler_params=pltpu.CompilerParams(vmem_limit_bytes=12 * MIB),
        name="attend",
    )(place, valid_pages, queried, page_scales.T, blocks, in_hbm(kv_pages))


def far_shapes(share, entry, groups):
    return (
        partial_of(share + small_count(share) + groups // 2 * entry),
        partial_of(groups // 2 * entry),
    )


def merge_near(place, pieces, share, block_rows, groups):
    entry = len(pieces) * block_rows
    return pl.pallas_call(
        lambda *refs: merge_near_kernel(share, block_rows, groups, *refs),
        in_specs=[SMEM] + [VMEM] * len(pieces),
        out_specs=(VMEM, VMEM),
        out_shape=far_shapes(share, entry, groups),
        scratch_shapes=[pltpu.VMEM((groups, entry, HEAD_SIZE), jnp.float32)],
        compiler_params=pltpu.CompilerParams(vmem_limit_bytes=4 * MIB),
        name="merge_near",
    )(place, *map(in_vmem, pieces))


def merge_mid(place, step, own, kept, got, share, entry, groups):
    return pl.pallas_call(
        lambda *refs: merge_mid_kernel(step, share, entry, *refs),
        in_specs=[SMEM] + [VMEM] * 3,
        out_specs=(VMEM, VMEM),
        out_shape=far_shapes(share, entry, groups),
        scratch_shapes=[pltpu.VMEM((groups, entry, HEAD_SIZE), jnp.float32)],
        compiler_params=pltpu.CompilerParams(vmem_limit_bytes=4 * MIB),
        name="merge_mid",
    )(place, *map(in_vmem, (own, kept, got)))


def merge_far(place, step, parents, queried, branch_kv, own, kept, got, share, entry, groups):
    units = share // queried.shape[2]
    return pl.pallas_call(
        lambda *refs: merge_far_kernel(units, step, entry, *refs),
        in_specs=[SMEM, SMEM] + [VMEM] * 5,
        out_specs=(VMEM, VMEM),
        out_shape=(partial_of(share), partial_of(groups * entry)),
        scratch_shapes=[pltpu.VMEM((groups, entry, HEAD_SIZE), jnp.float32)],
        compiler_params=pltpu.CompilerParams(vmem_limit_bytes=4 * MIB),
        name="merge_far",
    )(place, parents, queried, branch_kv, *map(in_vmem, (own, kept, got)))


def assemble(place, pieces, units):
    return pl.pallas_call(
        lambda *refs: assemble_kernel(units, *refs),
        in_specs=[SMEM] + [VMEM] * len(pieces),
        out_specs=VMEM,
        out_shape=jax.ShapeDtypeStruct((LAYERS, BEAMS, HQ * HEAD_SIZE), jnp.float32),
        compiler_params=pltpu.CompilerParams(vmem_limit_bytes=4 * MIB),
        name="assemble",
    )(place, *map(in_vmem, pieces))


def bits_of(devices):
    masks, mask = [], 1
    while mask < devices:
        masks.append(mask)
        mask *= 2
    return masks


def swap(array, mask, devices):
    return lax.ppermute(array, "seq", [(i, i ^ mask) for i in range(devices)])


def exchange_pages(pages):
    return lax.all_to_all(pages, "seq", split_axis=0, concat_axis=0, tiled=True)


def on_device(queries, kv_pages, page_scales, page_owner, valid_pages, branch_kv, parents):
    devices = lax.axis_size("seq")
    page_count = kv_pages.shape[0]
    slot_count = max(2, (page_count + devices - 1) // devices)
    first_slots = max(1, int(slot_count * FIRST_PART))
    own_max = slot_count * min(devices, page_count)
    group_size = HQ // KEY_VALUE_HEADS
    rows = LAYERS * BEAMS * HQ
    send_first = pack_first(kv_pages, page_owner, valid_pages, devices, first_slots)
    send_rest, send_scales = pack_rest(kv_pages, page_scales, page_owner, valid_pages, devices, slot_count, first_slots)
    recv_first = exchange_pages(send_first)
    recv_rest = exchange_pages(send_rest)

    me = lax.axis_index("seq")
    masks = bits_of(devices)
    inner = 2 * masks[(len(masks) - 1) // 2]
    groups = devices // inner
    share = rows // inner
    place = jnp.stack([me % inner, me // inner]).astype(jnp.int32)
    block_size = slot_count * page_scales.shape[1]
    block_rows = -(-block_size // HEAD_SIZE)
    blocks = send_scales.reshape(devices, block_size)
    blocks = jnp.pad(blocks, ((0, 0), (0, block_rows * HEAD_SIZE - block_size)))
    blocks = blocks.reshape(groups, inner, block_rows, HEAD_SIZE)
    queried = queries.reshape(LAYERS, BEAMS, KEY_VALUE_HEADS, group_size, HEAD_SIZE).swapaxes(1, 2)
    queried = queried.reshape(LAYERS, KEY_VALUE_HEADS, BEAMS * group_size, HEAD_SIZE)
    pieces = attend(place, queried, kv_pages, page_scales, valid_pages, blocks)

    def spread(parts, masks):
        return [parts[0]] + [swap(part, mask, devices) for part, mask in zip(parts[1:], masks)]

    pieces = spread(pieces, range(1, inner))
    own, kept = merge_near(place, pieces, share, block_rows, groups)
    entry = inner * block_rows
    far_masks = [mask for mask in masks if mask >= inner]
    for step, mask in enumerate(far_masks):
        got = swap(own, mask, devices)
        if mask != far_masks[-1]:
            own, kept = merge_mid(place, step, own, kept, got, share, entry, groups)
    mine, blocks = merge_far(
        place, len(far_masks) - 1, parents, queried, branch_kv, own, kept, got, share, entry, groups
    )
    pieces = spread([mine] * inner, range(1, inner))
    attended = assemble(place, pieces, share // (BEAMS * group_size))
    blocks = blocks.reshape(devices, block_rows * HEAD_SIZE)[:, :block_size]
    recv_scales = blocks.reshape(devices * slot_count, page_scales.shape[1]).astype(page_scales.dtype)
    counts = jnp.sum((recv_scales[:, 0] > 0).astype(jnp.int32).reshape(devices, slot_count), axis=1)
    page_cache, cache_scales_t = unpack_first(recv_first, recv_scales, counts, own_max)
    page_cache = unpack_rest(recv_rest, counts, page_cache, first_slots)
    return (page_cache, cache_scales_t.T, attended)


def solution(mesh):
    return jax.shard_map(
        on_device,
        mesh=mesh,
        in_specs=(P(), P("seq", None, None, None), P("seq", None), P("seq"), P("seq"), P(), P()),
        out_specs=(P("seq", None, None, None), P("seq", None), P()),
        check_vma=False,
    )
```

time: 455 us -> 150 us (0.33)
  the two profiles are of different devices: /device:TPU:16 before, /device:TPU:0 now
where the time goes in v3:
time: 150 us; the launch traced here: 149 us
  waiting for transfers between devices  80.7 us (54%)
  starting transfers between devices  31 us (21%)
  Pallas kernels  29.7 us (20%)
  local copies, waits for them, and re-layouts  4.85 us (3%)
  other arithmetic  1.63 us (1%)
  between operations  1.5 us (1%)
    all_to_all x2, waiting for transfers between devices, exchange_pages(): return lax.all_to_all(pages, 'seq', split_axis=0, concat_axis=0, tiled=True)  65.6 us
    ppermute x16, starting transfers between devices, swap(): return lax.ppermute(array, 'seq', [(i, i ^ mask) for i in range(devices)])  19.5 us
    ppermute x16, waiting for transfers between devices, swap(): return lax.ppermute(array, 'seq', [(i, i ^ mask) for i in range(devices)])  15.2 us
    all_to_all x2, starting transfers between devices, exchange_pages(): return lax.all_to_all(pages, 'seq', split_axis=0, concat_axis=0, tiled=True)  11.5 us
    pallas_call x1, Pallas kernels, attend(): pl.pallas_call(lambda *refs: attend_kernel(units, *refs), in_specs=[SMEM,...  9.36 us
    pallas_call x1, Pallas kernels, pack_rest(): pl.pallas_call(lambda *refs: pack_rest_kernel(first_slots, slot_count, *r...  5.06 us
    pallas_call x1, Pallas kernels, pack_first(): pl.pallas_call(lambda *refs: pack_first_kernel(slots, *refs), out_shape=p...  4.16 us
    pallas_call x1, Pallas kernels, unpack_first(): pl.pallas_call(lambda *refs: unpack_first_kernel(*refs), out_shape=(jax.S...  3.69 us
  transfers between devices with their start and end apart: 18, of which 8 were waited for; matrix products, arithmetic and copies ran while one was open for 3% of the time, Pallas kernels for 15%

profile of v3, /device:TPU:0, one launch (start us, length us, event | category | flops | bytes accessed | tf_op | source)
XLA Modules:
  0.0 149.4 jit_solution(6728072072085957813)
XLA Ops:
  2.0 4.2 %pack_first.1 = bf16[192,4,2,1024]{3,2,1,0:T(2,128)(2,1)} custom-call(s32[1]{0:T(128)S(6)} %copy.16.refs_0_.refs_1_, s32[1,256]{1,0:T(1,128)S(1)} %bitcast.17, bf16[256,4,2,1024]{3,2,1,0:T(2,128)(2,1)} %refs_2_.1), custom_call_target="tpu_custom_call" | custom-call | tf_op jit(solution)/shard_map/pack_first/pallas_call | solution.py:199
  6.1 7.3 %all-to-all-start.1 = ((bf16[192,4,2,1024]{3,2,1,0:T(2,128)(2,1)}), bf16[192,4,2,1024]{3,2,1,0:T(2,128)(2,1)S(1)}, u32[]{:S(2)}, u32[]{:S(2)}) async-start(bf16[192,4,2,1024]{3,2,1,0:T(2,128)(2,1)} %pack_first.1), calls=%async_computation.1 | async-start | bytes 6291456 | tf_op jit(solution)/shard_map/all_to_all | solution.py:571
  13.5 5.1 %pack_rest.1 = (bf16[64,4,2,1024]{3,2,1,0:T(2,128)(2,1)}, f32[256,32]{1,0:T(8,128)S(1)}) custom-call(s32[1]{0:T(128)S(6)} %copy.16.refs_0_.refs_1_, s32[1,256]{1,0:T(1,128)S(1)} %bitcast.18, bf16[32,256]{1,0:T(8,128)(2,1)S(1)} %bitcast.14, bf16[256,4,2,1024]{3,2,1,0:T(2,128)(2,1)} %refs_2_.1), custom_call_target="tpu_custom_call" | custom-call | tf_op jit(solution)/shard_map/pack_rest/pallas_call | solution.py:213
  19.2 65.6 %all-to-all-done.1.refs_3_ = bf16[192,4,2,1024]{3,2,1,0:T(2,128)(2,1)S(1)} async-done(((bf16[192,4,2,1024]{3,2,1,0:T(2,128)(2,1)}), bf16[192,4,2,1024]{3,2,1,0:T(2,128)(2,1)S(1)}, u32[]{:S(2)}, u32[]{:S(2)}) %all-to-all-start.1) | async-done | bytes 3145760 | tf_op jit(solution)/shard_map/all_to_all | solution.py:571
  84.8 4.2 %all-to-all-start = ((bf16[64,4,2,1024]{3,2,1,0:T(2,128)(2,1)}), bf16[64,4,2,1024]{3,2,1,0:T(2,128)(2,1)}, u32[]{:S(2)}, u32[]{:S(2)}) async-start(bf16[64,4,2,1024]{3,2,1,0:T(2,128)(2,1)} %get-tuple-element.35), calls=%async_computation | async-start | bytes 2097152 | tf_op jit(solution)/shard_map/all_to_all | solution.py:571
  91.1 9.4 %attend.1 = (f32[138,128]{1,0:T(8,128)S(1)}, f32[138,128]{1,0:T(8,128)S(1)}, f32[138,128]{1,0:T(8,128)S(1)}, f32[138,128]{1,0:T(8,128)S(1)}, f32[138,128]{1,0:T(...) custom-call(s32[2]{0:T(128)S(1)} %pad_add_fusion.refs_0_, ...), custom_call_target="tpu_custom_call" | custom-call | tf_op jit(solution)/shard_map/attend/pallas_call | solution.py:487
  100.7 1.6 %collective-permute-start.1 = (f32[138,128]{1,0:T(8,128)S(1)}, f32[138,128]{1,0:T(8,128)S(1)}, u32[]{:S(2)}, u32[]{:S(2)}) collective-permute-start(f32[138,128]{1,0:T(8,128)S(1)} %get-tuple-element.24), channel_id=1, source_target_pairs={{0,2},{1,3},{2,0},{3,1},{4,6},{5,7},{6,4},{7,5},{8,10},{9,11},{10,... | collective-permute-start | bytes 211976 | tf_op jit(solution)/shard_map/ppermute | solution.py:567
  102.4 1.7 %collective-permute-start.3 = (f32[138,128]{1,0:T(8,128)S(1)}, f32[138,128]{1,0:T(8,128)S(1)}, u32[]{:S(2)}, u32[]{:S(2)}) collective-permute-start(f32[138,128]{1,0:T(8,128)S(1)} %get-tuple-element.26), channel_id=1, source_target_pairs={{0,4},{1,5},{2,6},{3,7},{4,0},{5,1},{6,2},{7,3},{8,12},{9,13},{10,... | collective-permute-start | bytes 211976 | tf_op jit(solution)/shard_map/ppermute | solution.py:567
  104.2 2.5 %collective-permute-start.5 = (f32[138,128]{1,0:T(8,128)S(1)}, f32[138,128]{1,0:T(8,128)S(1)}, u32[]{:S(2)}, u32[]{:S(2)}) collective-permute-start(f32[138,128]{1,0:T(8,128)S(1)} %get-tuple-element.28), channel_id=1, source_target_pairs={{0,6},{1,7},{2,4},{3,5},{4,2},{5,3},{6,0},{7,1},{8,14},{9,15},{10,... | collective-permute-start | bytes 211976 | tf_op jit(solution)/shard_map/ppermute | solution.py:567
  107.9 1.3 collective-permute-done.3.refs_5_
  109.2 3.9 %collective-permute-done.4.refs_6_ = f32[138,128]{1,0:T(8,128)S(1)} collective-permute-done((f32[138,128]{1,0:T(8,128)S(1)}, f32[138,128]{1,0:T(8,128)S(1)}, u32[]{:S(2)}, u32[]{:S(2)}) %collective-permute-start.4) | collective-permute-done | bytes 70688 | tf_op jit(solution)/shard_map/ppermute | solution.py:567
  113.9 3.3 %collective-permute-start.7 = (f32[162,128]{1,0:T(8,128)S(1)}, f32[162,128]{1,0:T(8,128)S(1)}, u32[]{:S(2)}, u32[]{:S(2)}) collective-permute-start(f32[162,128]{1,0:T(8,128)S(1)} %get-tuple-element.30.refs_1_), channel_id=1, source_target_pairs={{0,8},{1,9},{2,10},{3,11},{4,12},{5,13},{6,14},{7,15},{8,0},{9,1},... | collective-permute-start | bytes 248840 | tf_op jit(solution)/shard_map/ppermute | solution.py:567
  117.2 2.8 %collective-permute-done.7.refs_3_ = f32[162,128]{1,0:T(8,128)S(1)} collective-permute-done((f32[162,128]{1,0:T(8,128)S(1)}, f32[162,128]{1,0:T(8,128)S(1)}, u32[]{:S(2)}, u32[]{:S(2)}) %collective-permute-start.7) | collective-permute-done | bytes 82976 | tf_op jit(solution)/shard_map/ppermute | solution.py:567
  120.7 2.6 %collective-permute-start.8 = (f32[162,128]{1,0:T(8,128)S(1)}, f32[162,128]{1,0:T(8,128)S(1)}, u32[]{:S(2)}, u32[]{:S(2)}) collective-permute-start(f32[162,128]{1,0:T(8,128)S(1)} %get-tuple-element.32.refs_4_), channel_id=1, source_target_pairs={{0,16},{1,17},{2,18},{3,19},{4,20},{5,21},{6,22},{7,23},{8,24},{9,... | collective-permute-start | bytes 248840 | tf_op jit(solution)/shard_map/ppermute | solution.py:567
  123.3 4.5 %collective-permute-done.8.refs_6_ = f32[162,128]{1,0:T(8,128)S(1)} collective-permute-done((f32[162,128]{1,0:T(8,128)S(1)}, f32[162,128]{1,0:T(8,128)S(1)}, u32[]{:S(2)}, u32[]{:S(2)}) %collective-permute-start.8) | collective-permute-done | bytes 82976 | tf_op jit(solution)/shard_map/ppermute | solution.py:567
  127.8 1.6 %merge_far.1 = (f32[128,128]{1,0:T(8,128)}, f32[64,128]{1,0:T(8,128)S(1)}) custom-call(s32[2]{0:T(128)S(1)} %pad_add_fusion.refs_0_, s32[8]{0:T(128)S(1)} %copy-done.5, bf16[2,8,64,128]{3,2,1,0:T(8,128)(2,1)S(1)} %bitcast.13, bf16[2,2,8,1024]{3,2,1,0:T(8,128)(2,1)S(1)} %copy-done.2, f32[162,128]{1,0:T(8,128)S(1)} %get-tuple-element.32.refs_4_, ...), custom_call_target="tpu_custom_call" | custom-call | tf_op jit(solution)/shard_map/merge_far/pallas_call | solution.py:536
  129.9 1.3 collective-permute-start.11
  134.3 1.8 %collective-permute-start.14 = (f32[128,128]{1,0:T(8,128)}, f32[128,128]{1,0:T(8,128)}, u32[]{:S(2)}, u32[]{:S(2)}) collective-permute-start(f32[128,128]{1,0:T(8,128)} %get-tuple-element.38.refs_1_), channel_id=1, source_target_pairs={{0,6},{1,7},{2,4},{3,5},{4,2},{5,3},{6,0},{7,1},{8,14},{9,15},{10,... | collective-permute-start | bytes 196616 | tf_op jit(solution)/shard_map/ppermute | solution.py:567
  136.0 1.0 collective-permute-start.15
  138.8 1.3 collective-permute-done.14.refs_7_
  140.0 1.2 collective-permute-done.15.refs_8_
  141.2 2.0 %assemble.1 = f32[2,8,8192]{2,1,0:T(8,128)} custom-call(s32[2]{0:T(128)S(1)} %pad_add_fusion.refs_0_, f32[128,128]{1,0:T(8,128)} %get-tuple-element.38.refs_1_, f32[128,128]{1,0:T(8,128)S(1)} %collective-permute-done.9.refs_2_, f32[128,128]{1,0:T(8,128)S(1)} %collective-permute-done.10.refs_3_, f32[128,128]{1,0:T(8,128)S(1)} %collective-permute-done.11.refs_4_, ...), custom_call_target="tpu_custom_call" | custom-call | tf_op jit(solution)/shard_map/assemble/pallas_call | solution.py:548
  143.2 3.7 %unpack_first.1 = (bf16[256,4,2,1024]{3,2,1,0:T(2,128)(2,1)}, bf16[32,256]{1,0:T(8,128)(2,1)}) custom-call(s32[32]{0:T(128)S(1)} %reduce_sum.9.refs_0_, s32[1,256]{1,0:T(1,128)S(1)} %bitcast.16, bf16[256,32]{1,0:T(8,128)(2,1)S(1)} %convert_element_type.30.refs_2_, bf16[192,4,2,1024]{3,2,1,0:T(2,128)(2,1)S(1)} %all-to-all-done.1.refs_3_), custom_call_target="tpu_custom_call" | custom-call | tf_op jit(solution)/shard_map/unpack_first/pallas_call | solution.py:230
  146.9 2.5 %unpack_rest.1 = bf16[256,4,2,1024]{3,2,1,0:T(2,128)(2,1)} custom-call(s32[32]{0:T(128)S(1)} %reduce_sum.9.refs_0_, bf16[64,4,2,1024]{3,2,1,0:T(2,128)(2,1)} %all-to-all-done.refs_1_, bf16[256,4,2,1024]{3,2,1,0:T(2,128)(2,1)} %get-tuple-element.36.refs_2_), custom_call_target="tpu_custom_call", output_to_operand_aliasing={{}: (2, {})} | custom-call | tf_op jit(solution)/shard_map/unpack_rest/pallas_call | solution.py:249
  (41 shorter events, 11.6 us)
Async XLA Ops:
  1.3 0.7 copy-start.3
  6.1 7.4 %copy-start.1 = (bf16[256,32]{0,1:T(8,128)(2,1)S(1)}, bf16[256,32]{0,1:T(8,128)(2,1)}, u32[]{:S(2)}) copy-start(bf16[256,32]{0,1:T(8,128)(2,1)} %param.9) | copy-start | bytes 49156
  6.1 7.4 %copy-start.4 = (s32[256]{0:T(256)S(1)}, s32[256]{0:T(256)}, u32[]{:S(2)}) copy-start(s32[256]{0:T(256)} %param.10) | copy-start | bytes 3076
  6.1 78.7 %all-to-all-start.1 = ((bf16[192,4,2,1024]{3,2,1,0:T(2,128)(2,1)}), bf16[192,4,2,1024]{3,2,1,0:T(2,128)(2,1)S(1)}, u32[]{:S(2)}, u32[]{:S(2)}) async-start(bf16[192,4,2,1024]{3,2,1,0:T(2,128)(2,1)} %pack_first.1), calls=%async_computation.1 | async-start | bytes 6291456 | tf_op jit(solution)/shard_map/all_to_all | solution.py:571
  18.6 0.7 copy-start
  19.2 108.5 %copy-start.2 = (bf16[2,2,8,1024]{3,2,1,0:T(8,128)(2,1)S(1)}, bf16[2,2,8,1024]{3,2,1,0:T(8,128)(2,1)}, u32[]{:S(2)}) copy-start(bf16[2,2,8,1024]{3,2,1,0:T(8,128)(2,1)} %refs_3_.3) | copy-start | bytes 196612
  19.2 108.5 %copy-start.5 = (s32[8]{0:T(128)S(1)}, s32[8]{0:T(128)}, u32[]{:S(2)}) copy-start(s32[8]{0:T(128)} %refs_1_.2) | copy-start | bytes 100
  84.8 62.1 %all-to-all-start = ((bf16[64,4,2,1024]{3,2,1,0:T(2,128)(2,1)}), bf16[64,4,2,1024]{3,2,1,0:T(2,128)(2,1)}, u32[]{:S(2)}, u32[]{:S(2)}) async-start(bf16[64,4,2,1024]{3,2,1,0:T(2,128)(2,1)} %get-tuple-element.35), calls=%async_computation | async-start | bytes 2097152 | tf_op jit(solution)/shard_map/all_to_all | solution.py:571
  100.5 3.7 %collective-permute-start = (f32[138,128]{1,0:T(8,128)S(1)}, f32[138,128]{1,0:T(8,128)S(1)}, u32[]{:S(2)}, u32[]{:S(2)}) collective-permute-start(f32[138,128]{1,0:T(8,128)S(1)} %get-tuple-element.23), channel_id=1, source_target_pairs={{0,1},{1,0},{2,3},{3,2},{4,5},{5,4},{6,7},{7,6},{8,9},{9,8},{10,11... | collective-permute-start | bytes 211976 | tf_op jit(solution)/shard_map/ppermute | solution.py:567
  100.7 6.1 %collective-permute-start.1 = (f32[138,128]{1,0:T(8,128)S(1)}, f32[138,128]{1,0:T(8,128)S(1)}, u32[]{:S(2)}, u32[]{:S(2)}) collective-permute-start(f32[138,128]{1,0:T(8,128)S(1)} %get-tuple-element.24), channel_id=1, source_target_pairs={{0,2},{1,3},{2,0},{3,1},{4,6},{5,7},{6,4},{7,5},{8,10},{9,11},{10,... | collective-permute-start | bytes 211976 | tf_op jit(solution)/shard_map/ppermute | solution.py:567
  102.4 5.5 %collective-permute-start.2 = (f32[138,128]{1,0:T(8,128)S(1)}, f32[138,128]{1,0:T(8,128)S(1)}, u32[]{:S(2)}, u32[]{:S(2)}) collective-permute-start(f32[138,128]{1,0:T(8,128)S(1)} %get-tuple-element.25), channel_id=1, source_target_pairs={{0,3},{1,2},{2,1},{3,0},{4,7},{5,6},{6,5},{7,4},{8,11},{9,10},{10,... | collective-permute-start | bytes 211976 | tf_op jit(solution)/shard_map/ppermute | solution.py:567
  102.4 6.8 %collective-permute-start.3 = (f32[138,128]{1,0:T(8,128)S(1)}, f32[138,128]{1,0:T(8,128)S(1)}, u32[]{:S(2)}, u32[]{:S(2)}) collective-permute-start(f32[138,128]{1,0:T(8,128)S(1)} %get-tuple-element.26), channel_id=1, source_target_pairs={{0,4},{1,5},{2,6},{3,7},{4,0},{5,1},{6,2},{7,3},{8,12},{9,13},{10,... | collective-permute-start | bytes 211976 | tf_op jit(solution)/shard_map/ppermute | solution.py:567
  104.1 9.0 %collective-permute-start.4 = (f32[138,128]{1,0:T(8,128)S(1)}, f32[138,128]{1,0:T(8,128)S(1)}, u32[]{:S(2)}, u32[]{:S(2)}) collective-permute-start(f32[138,128]{1,0:T(8,128)S(1)} %get-tuple-element.27), channel_id=1, source_target_pairs={{0,5},{1,4},{2,7},{3,6},{4,1},{5,0},{6,3},{7,2},{8,13},{9,12},{10,... | collective-permute-start | bytes 211976 | tf_op jit(solution)/shard_map/ppermute | solution.py:567
  104.2 8.9 %collective-permute-start.5 = (f32[138,128]{1,0:T(8,128)S(1)}, f32[138,128]{1,0:T(8,128)S(1)}, u32[]{:S(2)}, u32[]{:S(2)}) collective-permute-start(f32[138,128]{1,0:T(8,128)S(1)} %get-tuple-element.28), channel_id=1, source_target_pairs={{0,6},{1,7},{2,4},{3,5},{4,2},{5,3},{6,0},{7,1},{8,14},{9,15},{10,... | collective-permute-start | bytes 211976 | tf_op jit(solution)/shard_map/ppermute | solution.py:567
  106.9 6.3 %collective-permute-start.6 = (f32[138,128]{1,0:T(8,128)S(1)}, f32[138,128]{1,0:T(8,128)S(1)}, u32[]{:S(2)}, u32[]{:S(2)}) collective-permute-start(f32[138,128]{1,0:T(8,128)S(1)} %get-tuple-element.29), channel_id=1, source_target_pairs={{0,7},{1,6},{2,5},{3,4},{4,3},{5,2},{6,1},{7,0},{8,15},{9,14},{10,... | collective-permute-start | bytes 211976 | tf_op jit(solution)/shard_map/ppermute | solution.py:567
  113.9 6.1 %collective-permute-start.7 = (f32[162,128]{1,0:T(8,128)S(1)}, f32[162,128]{1,0:T(8,128)S(1)}, u32[]{:S(2)}, u32[]{:S(2)}) collective-permute-start(f32[162,128]{1,0:T(8,128)S(1)} %get-tuple-element.30.refs_1_), channel_id=1, source_target_pairs={{0,8},{1,9},{2,10},{3,11},{4,12},{5,13},{6,14},{7,15},{8,0},{9,1},... | collective-permute-start | bytes 248840 | tf_op jit(solution)/shard_map/ppermute | solution.py:567
  120.7 7.1 %collective-permute-start.8 = (f32[162,128]{1,0:T(8,128)S(1)}, f32[162,128]{1,0:T(8,128)S(1)}, u32[]{:S(2)}, u32[]{:S(2)}) collective-permute-start(f32[162,128]{1,0:T(8,128)S(1)} %get-tuple-element.32.refs_4_), channel_id=1, source_target_pairs={{0,16},{1,17},{2,18},{3,19},{4,20},{5,21},{6,22},{7,23},{8,24},{9,... | collective-permute-start | bytes 248840 | tf_op jit(solution)/shard_map/ppermute | solution.py:567
  129.3 4.9 %collective-permute-start.9 = (f32[128,128]{1,0:T(8,128)}, f32[128,128]{1,0:T(8,128)S(1)}, u32[]{:S(2)}, u32[]{:S(2)}) collective-permute-start(f32[128,128]{1,0:T(8,128)} %get-tuple-element.38.refs_1_), channel_id=1, source_target_pairs={{0,1},{1,0},{2,3},{3,2},{4,5},{5,4},{6,7},{7,6},{8,9},{9,8},{10,11... | collective-permute-start | bytes 196616 | tf_op jit(solution)/shard_map/ppermute | solution.py:567
  129.3 6.7 %collective-permute-start.10 = (f32[128,128]{1,0:T(8,128)}, f32[128,128]{1,0:T(8,128)S(1)}, u32[]{:S(2)}, u32[]{:S(2)}) collective-permute-start(f32[128,128]{1,0:T(8,128)} %get-tuple-element.38.refs_1_), channel_id=1, source_target_pairs={{0,2},{1,3},{2,0},{3,1},{4,6},{5,7},{6,4},{7,5},{8,10},{9,11},{10,... | collective-permute-start | bytes 196616 | tf_op jit(solution)/shard_map/ppermute | solution.py:567
  129.9 8.9 %collective-permute-start.11 = (f32[128,128]{1,0:T(8,128)}, f32[128,128]{1,0:T(8,128)S(1)}, u32[]{:S(2)}, u32[]{:S(2)}) collective-permute-start(f32[128,128]{1,0:T(8,128)} %get-tuple-element.38.refs_1_), channel_id=1, source_target_pairs={{0,3},{1,2},{2,1},{3,0},{4,7},{5,6},{6,5},{7,4},{8,11},{9,10},{10,... | collective-permute-start | bytes 196616 | tf_op jit(solution)/shard_map/ppermute | solution.py:567
  131.2 7.5 %collective-permute-start.12 = (f32[128,128]{1,0:T(8,128)}, f32[128,128]{1,0:T(8,128)S(1)}, u32[]{:S(2)}, u32[]{:S(2)}) collective-permute-start(f32[128,128]{1,0:T(8,128)} %get-tuple-element.38.refs_1_), channel_id=1, source_target_pairs={{0,4},{1,5},{2,6},{3,7},{4,0},{5,1},{6,2},{7,3},{8,12},{9,13},{10,... | collective-permute-start | bytes 196616 | tf_op jit(solution)/shard_map/ppermute | solution.py:567
  132.1 6.7 %collective-permute-start.13 = (f32[128,128]{1,0:T(8,128)}, f32[128,128]{1,0:T(8,128)S(1)}, u32[]{:S(2)}, u32[]{:S(2)}) collective-permute-start(f32[128,128]{1,0:T(8,128)} %get-tuple-element.38.refs_1_), channel_id=1, source_target_pairs={{0,5},{1,4},{2,7},{3,6},{4,1},{5,0},{6,3},{7,2},{8,13},{9,12},{10,... | collective-permute-start | bytes 196616 | tf_op jit(solution)/shard_map/ppermute | solution.py:567
  134.3 5.8 %collective-permute-start.14 = (f32[128,128]{1,0:T(8,128)}, f32[128,128]{1,0:T(8,128)}, u32[]{:S(2)}, u32[]{:S(2)}) collective-permute-start(f32[128,128]{1,0:T(8,128)} %get-tuple-element.38.refs_1_), channel_id=1, source_target_pairs={{0,6},{1,7},{2,4},{3,5},{4,2},{5,3},{6,0},{7,1},{8,14},{9,15},{10,... | collective-permute-start | bytes 196616 | tf_op jit(solution)/shard_map/ppermute | solution.py:567
  136.0 5.2 %collective-permute-start.15 = (f32[128,128]{1,0:T(8,128)}, f32[128,128]{1,0:T(8,128)}, u32[]{:S(2)}, u32[]{:S(2)}) collective-permute-start(f32[128,128]{1,0:T(8,128)} %get-tuple-element.38.refs_1_), channel_id=1, source_target_pairs={{0,7},{1,6},{2,5},{3,4},{4,3},{5,2},{6,1},{7,0},{8,15},{9,14},{10,... | collective-permute-start | bytes 196616 | tf_op jit(solution)/shard_map/ppermute | solution.py:567

commit v4 on v3

--- a/solution.py
+++ b/solution.py
@@ -148,26 +148,21 @@
     fetches = [pltpu.make_async_copy(recv_pages.at[part], held.at[part], in_sems.at[c]) for c, part in enumerate(parts)]
     for fetch in fetches:
         fetch.start()
-
-    def keep(source, carry):
-        row, copied = carry
-        count = counts_s[source]
-
-        def one(slot, inner):
-            pltpu.make_async_copy(
-                held.at[source * rest_slots + slot], page_cache.at[row + first_slots + slot], sem
-            ).start()
-            return inner
-
-        here = jnp.maximum(count - first_slots, 0)
-        lax.fori_loop(0, here, one, 0)
-        return row + count, copied + here
-
-    carry = (0, 0)
+    row, copied = 0, 0
     for c, fetch in enumerate(fetches):
         fetch.wait()
-        carry = lax.fori_loop(c * size // rest_slots, (c + 1) * size // rest_slots, keep, carry)
-    wait_pages(carry[1], page_cache, sem)
+        for source in range(c * size // rest_slots, (c + 1) * size // rest_slots):
+            count = counts_s[source]
+            for slot in range(rest_slots):
+                first = row + first_slots + slot
+
+                @pl.when(count > first_slots + slot)
+                def _():
+                    pltpu.make_async_copy(held.at[source * rest_slots + slot], page_cache.at[first], sem).start()
+
+            row += count
+            copied += jnp.maximum(count - first_slots, 0)
+    wait_pages(copied, page_cache, sem)
 
 
 ANY = pl.BlockSpec(memory_space=pl.ANY)
@@ -241,7 +236,7 @@
         ],
         compiler_params=pltpu.CompilerParams(vmem_limit_bytes=4 * MIB),
         name="unpack_first",
-    )(counts, used.reshape(1, slots), recv_scales, in_vmem(recv_pages))
+    )(counts, used.reshape(1, slots), recv_scales, recv_pages)
 
 
 def unpack_rest(recv_pages, counts, page_cache, first_slots):

time: 150 us -> 150 us (level)
  no operation moved by 1% of the time
where the time goes in v4:
time: 150 us; the launch traced here: 149 us
  waiting for transfers between devices  80.7 us (54%)
  starting transfers between devices  31 us (21%)
  Pallas kernels  29.6 us (20%)
  local copies, waits for them, and re-layouts  4.85 us (3%)
  other arithmetic  1.63 us (1%)
  between operations  1.5 us (1%)
    all_to_all x2, waiting for transfers between devices, exchange_pages(): return lax.all_to_all(pages, 'seq', split_axis=0, concat_axis=0, tiled=True)  65.6 us
    ppermute x16, starting transfers between devices, swap(): return lax.ppermute(array, 'seq', [(i, i ^ mask) for i in range(devices)])  19.5 us
    ppermute x16, waiting for transfers between devices, swap(): return lax.ppermute(array, 'seq', [(i, i ^ mask) for i in range(devices)])  15.2 us
    all_to_all x2, starting transfers between devices, exchange_pages(): return lax.all_to_all(pages, 'seq', split_axis=0, concat_axis=0, tiled=True)  11.5 us
    pallas_call x1, Pallas kernels, attend(): pl.pallas_call(lambda *refs: attend_kernel(units, *refs), in_specs=[SMEM,...  9.36 us
    pallas_call x1, Pallas kernels, pack_rest(): pl.pallas_call(lambda *refs: pack_rest_kernel(first_slots, slot_count, *r...  5.06 us
    pallas_call x1, Pallas kernels, pack_first(): pl.pallas_call(lambda *refs: pack_first_kernel(slots, *refs), out_shape=p...  4.16 us
    pallas_call x1, Pallas kernels, unpack_first(): pl.pallas_call(lambda *refs: unpack_first_kernel(*refs), out_shape=(jax.S...  3.69 us
  transfers between devices with their start and end apart: 18, of which 8 were waited for; matrix products, arithmetic and copies ran while one was open for 3% of the time, Pallas kernels for 15%

profile of v4, /device:TPU:0, one launch (start us, length us, event | category | flops | bytes accessed | tf_op | source)
XLA Modules:
  0.0 149.3 jit_solution(1463988782181195263)
XLA Ops:
  2.0 4.2 %pack_first.1 = bf16[192,4,2,1024]{3,2,1,0:T(2,128)(2,1)} custom-call(s32[1]{0:T(128)S(6)} %copy.16.refs_0_.refs_1_, s32[1,256]{1,0:T(1,128)S(1)} %bitcast.17, bf16[256,4,2,1024]{3,2,1,0:T(2,128)(2,1)} %refs_2_.1), custom_call_target="tpu_custom_call" | custom-call | tf_op jit(solution)/shard_map/pack_first/pallas_call | solution.py:194
  6.1 7.3 %all-to-all-start.1 = ((bf16[192,4,2,1024]{3,2,1,0:T(2,128)(2,1)}), bf16[192,4,2,1024]{3,2,1,0:T(2,128)(2,1)S(1)}, u32[]{:S(2)}, u32[]{:S(2)}) async-start(bf16[192,4,2,1024]{3,2,1,0:T(2,128)(2,1)} %pack_first.1), calls=%async_computation.1 | async-start | bytes 6291456 | tf_op jit(solution)/shard_map/all_to_all | solution.py:566
  13.5 5.1 %pack_rest.1 = (bf16[64,4,2,1024]{3,2,1,0:T(2,128)(2,1)}, f32[256,32]{1,0:T(8,128)S(1)}) custom-call(s32[1]{0:T(128)S(6)} %copy.16.refs_0_.refs_1_, s32[1,256]{1,0:T(1,128)S(1)} %bitcast.18, bf16[32,256]{1,0:T(8,128)(2,1)S(1)} %bitcast.14, bf16[256,4,2,1024]{3,2,1,0:T(2,128)(2,1)} %refs_2_.1), custom_call_target="tpu_custom_call" | custom-call | tf_op jit(solution)/shard_map/pack_rest/pallas_call | solution.py:208
  19.2 65.6 %all-to-all-done.1.refs_3_ = bf16[192,4,2,1024]{3,2,1,0:T(2,128)(2,1)S(1)} async-done(((bf16[192,4,2,1024]{3,2,1,0:T(2,128)(2,1)}), bf16[192,4,2,1024]{3,2,1,0:T(2,128)(2,1)S(1)}, u32[]{:S(2)}, u32[]{:S(2)}) %all-to-all-start.1) | async-done | bytes 3145760 | tf_op jit(solution)/shard_map/all_to_all | solution.py:566
  84.8 4.2 %all-to-all-start = ((bf16[64,4,2,1024]{3,2,1,0:T(2,128)(2,1)}), bf16[64,4,2,1024]{3,2,1,0:T(2,128)(2,1)}, u32[]{:S(2)}, u32[]{:S(2)}) async-start(bf16[64,4,2,1024]{3,2,1,0:T(2,128)(2,1)} %get-tuple-element.35), calls=%async_computation | async-start | bytes 2097152 | tf_op jit(solution)/shard_map/all_to_all | solution.py:566
  91.1 9.4 %attend.1 = (f32[138,128]{1,0:T(8,128)S(1)}, f32[138,128]{1,0:T(8,128)S(1)}, f32[138,128]{1,0:T(8,128)S(1)}, f32[138,128]{1,0:T(8,128)S(1)}, f32[138,128]{1,0:T(...) custom-call(s32[2]{0:T(128)S(1)} %pad_add_fusion.refs_0_, ...), custom_call_target="tpu_custom_call" | custom-call | tf_op jit(solution)/shard_map/attend/pallas_call | solution.py:482
  100.7 1.6 %collective-permute-start.1 = (f32[138,128]{1,0:T(8,128)S(1)}, f32[138,128]{1,0:T(8,128)S(1)}, u32[]{:S(2)}, u32[]{:S(2)}) collective-permute-start(f32[138,128]{1,0:T(8,128)S(1)} %get-tuple-element.24), channel_id=1, source_target_pairs={{0,2},{1,3},{2,0},{3,1},{4,6},{5,7},{6,4},{7,5},{8,10},{9,11},{10,... | collective-permute-start | bytes 211976 | tf_op jit(solution)/shard_map/ppermute | solution.py:562
  102.4 1.7 %collective-permute-start.3 = (f32[138,128]{1,0:T(8,128)S(1)}, f32[138,128]{1,0:T(8,128)S(1)}, u32[]{:S(2)}, u32[]{:S(2)}) collective-permute-start(f32[138,128]{1,0:T(8,128)S(1)} %get-tuple-element.26), channel_id=1, source_target_pairs={{0,4},{1,5},{2,6},{3,7},{4,0},{5,1},{6,2},{7,3},{8,12},{9,13},{10,... | collective-permute-start | bytes 211976 | tf_op jit(solution)/shard_map/ppermute | solution.py:562
  104.2 2.5 %collective-permute-start.5 = (f32[138,128]{1,0:T(8,128)S(1)}, f32[138,128]{1,0:T(8,128)S(1)}, u32[]{:S(2)}, u32[]{:S(2)}) collective-permute-start(f32[138,128]{1,0:T(8,128)S(1)} %get-tuple-element.28), channel_id=1, source_target_pairs={{0,6},{1,7},{2,4},{3,5},{4,2},{5,3},{6,0},{7,1},{8,14},{9,15},{10,... | collective-permute-start | bytes 211976 | tf_op jit(solution)/shard_map/ppermute | solution.py:562
  107.9 1.3 collective-permute-done.3.refs_5_
  109.2 3.9 %collective-permute-done.4.refs_6_ = f32[138,128]{1,0:T(8,128)S(1)} collective-permute-done((f32[138,128]{1,0:T(8,128)S(1)}, f32[138,128]{1,0:T(8,128)S(1)}, u32[]{:S(2)}, u32[]{:S(2)}) %collective-permute-start.4) | collective-permute-done | bytes 70688 | tf_op jit(solution)/shard_map/ppermute | solution.py:562
  113.9 3.3 %collective-permute-start.7 = (f32[162,128]{1,0:T(8,128)S(1)}, f32[162,128]{1,0:T(8,128)S(1)}, u32[]{:S(2)}, u32[]{:S(2)}) collective-permute-start(f32[162,128]{1,0:T(8,128)S(1)} %get-tuple-element.30.refs_1_), channel_id=1, source_target_pairs={{0,8},{1,9},{2,10},{3,11},{4,12},{5,13},{6,14},{7,15},{8,0},{9,1},... | collective-permute-start | bytes 248840 | tf_op jit(solution)/shard_map/ppermute | solution.py:562
  117.2 2.8 %collective-permute-done.7.refs_3_ = f32[162,128]{1,0:T(8,128)S(1)} collective-permute-done((f32[162,128]{1,0:T(8,128)S(1)}, f32[162,128]{1,0:T(8,128)S(1)}, u32[]{:S(2)}, u32[]{:S(2)}) %collective-permute-start.7) | collective-permute-done | bytes 82976 | tf_op jit(solution)/shard_map/ppermute | solution.py:562
  120.7 2.6 %collective-permute-start.8 = (f32[162,128]{1,0:T(8,128)S(1)}, f32[162,128]{1,0:T(8,128)S(1)}, u32[]{:S(2)}, u32[]{:S(2)}) collective-permute-start(f32[162,128]{1,0:T(8,128)S(1)} %get-tuple-element.32.refs_4_), channel_id=1, source_target_pairs={{0,16},{1,17},{2,18},{3,19},{4,20},{5,21},{6,22},{7,23},{8,24},{9,... | collective-permute-start | bytes 248840 | tf_op jit(solution)/shard_map/ppermute | solution.py:562
  123.3 4.5 %collective-permute-done.8.refs_6_ = f32[162,128]{1,0:T(8,128)S(1)} collective-permute-done((f32[162,128]{1,0:T(8,128)S(1)}, f32[162,128]{1,0:T(8,128)S(1)}, u32[]{:S(2)}, u32[]{:S(2)}) %collective-permute-start.8) | collective-permute-done | bytes 82976 | tf_op jit(solution)/shard_map/ppermute | solution.py:562
  127.8 1.6 %merge_far.1 = (f32[128,128]{1,0:T(8,128)}, f32[64,128]{1,0:T(8,128)S(1)}) custom-call(s32[2]{0:T(128)S(1)} %pad_add_fusion.refs_0_, s32[8]{0:T(128)S(1)} %copy-done.5, bf16[2,8,64,128]{3,2,1,0:T(8,128)(2,1)S(1)} %bitcast.13, bf16[2,2,8,1024]{3,2,1,0:T(8,128)(2,1)S(1)} %copy-done.2, f32[162,128]{1,0:T(8,128)S(1)} %get-tuple-element.32.refs_4_, ...), custom_call_target="tpu_custom_call" | custom-call | tf_op jit(solution)/shard_map/merge_far/pallas_call | solution.py:531
  129.9 1.3 collective-permute-start.11
  134.3 1.8 %collective-permute-start.14 = (f32[128,128]{1,0:T(8,128)}, f32[128,128]{1,0:T(8,128)}, u32[]{:S(2)}, u32[]{:S(2)}) collective-permute-start(f32[128,128]{1,0:T(8,128)} %get-tuple-element.38.refs_1_), channel_id=1, source_target_pairs={{0,6},{1,7},{2,4},{3,5},{4,2},{5,3},{6,0},{7,1},{8,14},{9,15},{10,... | collective-permute-start | bytes 196616 | tf_op jit(solution)/shard_map/ppermute | solution.py:562
  136.0 1.0 collective-permute-start.15
  138.8 1.3 collective-permute-done.14.refs_7_
  140.0 1.2 collective-permute-done.15.refs_8_
  141.2 2.0 %assemble.1 = f32[2,8,8192]{2,1,0:T(8,128)} custom-call(s32[2]{0:T(128)S(1)} %pad_add_fusion.refs_0_, f32[128,128]{1,0:T(8,128)} %get-tuple-element.38.refs_1_, f32[128,128]{1,0:T(8,128)S(1)} %collective-permute-done.9.refs_2_, f32[128,128]{1,0:T(8,128)S(1)} %collective-permute-done.10.refs_3_, f32[128,128]{1,0:T(8,128)S(1)} %collective-permute-done.11.refs_4_, ...), custom_call_target="tpu_custom_call" | custom-call | tf_op jit(solution)/shard_map/assemble/pallas_call | solution.py:543
  143.2 3.7 %unpack_first.1 = (bf16[256,4,2,1024]{3,2,1,0:T(2,128)(2,1)}, bf16[32,256]{1,0:T(8,128)(2,1)}) custom-call(s32[32]{0:T(128)S(1)} %reduce_sum.9.refs_0_, s32[1,256]{1,0:T(1,128)S(1)} %bitcast.16, bf16[256,32]{1,0:T(8,128)(2,1)S(1)} %convert_element_type.30.refs_2_, bf16[192,4,2,1024]{3,2,1,0:T(2,128)(2,1)S(1)} %all-to-all-done.1.refs_3_), custom_call_target="tpu_custom_call" | custom-call | tf_op jit(solution)/shard_map/unpack_first/pallas_call | solution.py:225
  146.9 2.4 %unpack_rest.1 = bf16[256,4,2,1024]{3,2,1,0:T(2,128)(2,1)} custom-call(s32[32]{0:T(128)S(1)} %reduce_sum.9.refs_0_, bf16[64,4,2,1024]{3,2,1,0:T(2,128)(2,1)} %all-to-all-done.refs_1_, bf16[256,4,2,1024]{3,2,1,0:T(2,128)(2,1)} %get-tuple-element.36.refs_2_), custom_call_target="tpu_custom_call", output_to_operand_aliasing={{}: (2, {})} | custom-call | tf_op jit(solution)/shard_map/unpack_rest/pallas_call | solution.py:244
  (41 shorter events, 11.6 us)
Async XLA Ops:
  1.3 0.7 copy-start.3
  6.1 7.4 %copy-start.1 = (bf16[256,32]{0,1:T(8,128)(2,1)S(1)}, bf16[256,32]{0,1:T(8,128)(2,1)}, u32[]{:S(2)}) copy-start(bf16[256,32]{0,1:T(8,128)(2,1)} %param.9) | copy-start | bytes 49156
  6.1 7.4 %copy-start.4 = (s32[256]{0:T(256)S(1)}, s32[256]{0:T(256)}, u32[]{:S(2)}) copy-start(s32[256]{0:T(256)} %param.10) | copy-start | bytes 3076
  6.1 78.7 %all-to-all-start.1 = ((bf16[192,4,2,1024]{3,2,1,0:T(2,128)(2,1)}), bf16[192,4,2,1024]{3,2,1,0:T(2,128)(2,1)S(1)}, u32[]{:S(2)}, u32[]{:S(2)}) async-start(bf16[192,4,2,1024]{3,2,1,0:T(2,128)(2,1)} %pack_first.1), calls=%async_computation.1 | async-start | bytes 6291456 | tf_op jit(solution)/shard_map/all_to_all | solution.py:566
  18.6 0.7 copy-start
  19.2 108.5 %copy-start.2 = (bf16[2,2,8,1024]{3,2,1,0:T(8,128)(2,1)S(1)}, bf16[2,2,8,1024]{3,2,1,0:T(8,128)(2,1)}, u32[]{:S(2)}) copy-start(bf16[2,2,8,1024]{3,2,1,0:T(8,128)(2,1)} %refs_3_.3) | copy-start | bytes 196612
  19.2 108.5 %copy-start.5 = (s32[8]{0:T(128)S(1)}, s32[8]{0:T(128)}, u32[]{:S(2)}) copy-start(s32[8]{0:T(128)} %refs_1_.2) | copy-start | bytes 100
  84.8 62.1 %all-to-all-start = ((bf16[64,4,2,1024]{3,2,1,0:T(2,128)(2,1)}), bf16[64,4,2,1024]{3,2,1,0:T(2,128)(2,1)}, u32[]{:S(2)}, u32[]{:S(2)}) async-start(bf16[64,4,2,1024]{3,2,1,0:T(2,128)(2,1)} %get-tuple-element.35), calls=%async_computation | async-start | bytes 2097152 | tf_op jit(solution)/shard_map/all_to_all | solution.py:566
  100.5 3.7 %collective-permute-start = (f32[138,128]{1,0:T(8,128)S(1)}, f32[138,128]{1,0:T(8,128)S(1)}, u32[]{:S(2)}, u32[]{:S(2)}) collective-permute-start(f32[138,128]{1,0:T(8,128)S(1)} %get-tuple-element.23), channel_id=1, source_target_pairs={{0,1},{1,0},{2,3},{3,2},{4,5},{5,4},{6,7},{7,6},{8,9},{9,8},{10,11... | collective-permute-start | bytes 211976 | tf_op jit(solution)/shard_map/ppermute | solution.py:562
  100.7 6.1 %collective-permute-start.1 = (f32[138,128]{1,0:T(8,128)S(1)}, f32[138,128]{1,0:T(8,128)S(1)}, u32[]{:S(2)}, u32[]{:S(2)}) collective-permute-start(f32[138,128]{1,0:T(8,128)S(1)} %get-tuple-element.24), channel_id=1, source_target_pairs={{0,2},{1,3},{2,0},{3,1},{4,6},{5,7},{6,4},{7,5},{8,10},{9,11},{10,... | collective-permute-start | bytes 211976 | tf_op jit(solution)/shard_map/ppermute | solution.py:562
  102.4 5.5 %collective-permute-start.2 = (f32[138,128]{1,0:T(8,128)S(1)}, f32[138,128]{1,0:T(8,128)S(1)}, u32[]{:S(2)}, u32[]{:S(2)}) collective-permute-start(f32[138,128]{1,0:T(8,128)S(1)} %get-tuple-element.25), channel_id=1, source_target_pairs={{0,3},{1,2},{2,1},{3,0},{4,7},{5,6},{6,5},{7,4},{8,11},{9,10},{10,... | collective-permute-start | bytes 211976 | tf_op jit(solution)/shard_map/ppermute | solution.py:562
  102.4 6.8 %collective-permute-start.3 = (f32[138,128]{1,0:T(8,128)S(1)}, f32[138,128]{1,0:T(8,128)S(1)}, u32[]{:S(2)}, u32[]{:S(2)}) collective-permute-start(f32[138,128]{1,0:T(8,128)S(1)} %get-tuple-element.26), channel_id=1, source_target_pairs={{0,4},{1,5},{2,6},{3,7},{4,0},{5,1},{6,2},{7,3},{8,12},{9,13},{10,... | collective-permute-start | bytes 211976 | tf_op jit(solution)/shard_map/ppermute | solution.py:562
  104.1 9.0 %collective-permute-start.4 = (f32[138,128]{1,0:T(8,128)S(1)}, f32[138,128]{1,0:T(8,128)S(1)}, u32[]{:S(2)}, u32[]{:S(2)}) collective-permute-start(f32[138,128]{1,0:T(8,128)S(1)} %get-tuple-element.27), channel_id=1, source_target_pairs={{0,5},{1,4},{2,7},{3,6},{4,1},{5,0},{6,3},{7,2},{8,13},{9,12},{10,... | collective-permute-start | bytes 211976 | tf_op jit(solution)/shard_map/ppermute | solution.py:562
  104.2 8.9 %collective-permute-start.5 = (f32[138,128]{1,0:T(8,128)S(1)}, f32[138,128]{1,0:T(8,128)S(1)}, u32[]{:S(2)}, u32[]{:S(2)}) collective-permute-start(f32[138,128]{1,0:T(8,128)S(1)} %get-tuple-element.28), channel_id=1, source_target_pairs={{0,6},{1,7},{2,4},{3,5},{4,2},{5,3},{6,0},{7,1},{8,14},{9,15},{10,... | collective-permute-start | bytes 211976 | tf_op jit(solution)/shard_map/ppermute | solution.py:562
  106.9 6.3 %collective-permute-start.6 = (f32[138,128]{1,0:T(8,128)S(1)}, f32[138,128]{1,0:T(8,128)S(1)}, u32[]{:S(2)}, u32[]{:S(2)}) collective-permute-start(f32[138,128]{1,0:T(8,128)S(1)} %get-tuple-element.29), channel_id=1, source_target_pairs={{0,7},{1,6},{2,5},{3,4},{4,3},{5,2},{6,1},{7,0},{8,15},{9,14},{10,... | collective-permute-start | bytes 211976 | tf_op jit(solution)/shard_map/ppermute | solution.py:562
  113.9 6.1 %collective-permute-start.7 = (f32[162,128]{1,0:T(8,128)S(1)}, f32[162,128]{1,0:T(8,128)S(1)}, u32[]{:S(2)}, u32[]{:S(2)}) collective-permute-start(f32[162,128]{1,0:T(8,128)S(1)} %get-tuple-element.30.refs_1_), channel_id=1, source_target_pairs={{0,8},{1,9},{2,10},{3,11},{4,12},{5,13},{6,14},{7,15},{8,0},{9,1},... | collective-permute-start | bytes 248840 | tf_op jit(solution)/shard_map/ppermute | solution.py:562
  120.7 7.1 %collective-permute-start.8 = (f32[162,128]{1,0:T(8,128)S(1)}, f32[162,128]{1,0:T(8,128)S(1)}, u32[]{:S(2)}, u32[]{:S(2)}) collective-permute-start(f32[162,128]{1,0:T(8,128)S(1)} %get-tuple-element.32.refs_4_), channel_id=1, source_target_pairs={{0,16},{1,17},{2,18},{3,19},{4,20},{5,21},{6,22},{7,23},{8,24},{9,... | collective-permute-start | bytes 248840 | tf_op jit(solution)/shard_map/ppermute | solution.py:562
  129.3 4.9 %collective-permute-start.9 = (f32[128,128]{1,0:T(8,128)}, f32[128,128]{1,0:T(8,128)S(1)}, u32[]{:S(2)}, u32[]{:S(2)}) collective-permute-start(f32[128,128]{1,0:T(8,128)} %get-tuple-element.38.refs_1_), channel_id=1, source_target_pairs={{0,1},{1,0},{2,3},{3,2},{4,5},{5,4},{6,7},{7,6},{8,9},{9,8},{10,11... | collective-permute-start | bytes 196616 | tf_op jit(solution)/shard_map/ppermute | solution.py:562
  129.3 6.7 %collective-permute-start.10 = (f32[128,128]{1,0:T(8,128)}, f32[128,128]{1,0:T(8,128)S(1)}, u32[]{:S(2)}, u32[]{:S(2)}) collective-permute-start(f32[128,128]{1,0:T(8,128)} %get-tuple-element.38.refs_1_), channel_id=1, source_target_pairs={{0,2},{1,3},{2,0},{3,1},{4,6},{5,7},{6,4},{7,5},{8,10},{9,11},{10,... | collective-permute-start | bytes 196616 | tf_op jit(solution)/shard_map/ppermute | solution.py:562
  129.9 8.9 %collective-permute-start.11 = (f32[128,128]{1,0:T(8,128)}, f32[128,128]{1,0:T(8,128)S(1)}, u32[]{:S(2)}, u32[]{:S(2)}) collective-permute-start(f32[128,128]{1,0:T(8,128)} %get-tuple-element.38.refs_1_), channel_id=1, source_target_pairs={{0,3},{1,2},{2,1},{3,0},{4,7},{5,6},{6,5},{7,4},{8,11},{9,10},{10,... | collective-permute-start | bytes 196616 | tf_op jit(solution)/shard_map/ppermute | solution.py:562
  131.2 7.5 %collective-permute-start.12 = (f32[128,128]{1,0:T(8,128)}, f32[128,128]{1,0:T(8,128)S(1)}, u32[]{:S(2)}, u32[]{:S(2)}) collective-permute-start(f32[128,128]{1,0:T(8,128)} %get-tuple-element.38.refs_1_), channel_id=1, source_target_pairs={{0,4},{1,5},{2,6},{3,7},{4,0},{5,1},{6,2},{7,3},{8,12},{9,13},{10,... | collective-permute-start | bytes 196616 | tf_op jit(solution)/shard_map/ppermute | solution.py:562
  132.1 6.7 %collective-permute-start.13 = (f32[128,128]{1,0:T(8,128)}, f32[128,128]{1,0:T(8,128)S(1)}, u32[]{:S(2)}, u32[]{:S(2)}) collective-permute-start(f32[128,128]{1,0:T(8,128)} %get-tuple-element.38.refs_1_), channel_id=1, source_target_pairs={{0,5},{1,4},{2,7},{3,6},{4,1},{5,0},{6,3},{7,2},{8,13},{9,12},{10,... | collective-permute-start | bytes 196616 | tf_op jit(solution)/shard_map/ppermute | solution.py:562
  134.3 5.8 %collective-permute-start.14 = (f32[128,128]{1,0:T(8,128)}, f32[128,128]{1,0:T(8,128)}, u32[]{:S(2)}, u32[]{:S(2)}) collective-permute-start(f32[128,128]{1,0:T(8,128)} %get-tuple-element.38.refs_1_), channel_id=1, source_target_pairs={{0,6},{1,7},{2,4},{3,5},{4,2},{5,3},{6,0},{7,1},{8,14},{9,15},{10,... | collective-permute-start | bytes 196616 | tf_op jit(solution)/shard_map/ppermute | solution.py:562
  136.0 5.2 %collective-permute-start.15 = (f32[128,128]{1,0:T(8,128)}, f32[128,128]{1,0:T(8,128)}, u32[]{:S(2)}, u32[]{:S(2)}) collective-permute-start(f32[128,128]{1,0:T(8,128)} %get-tuple-element.38.refs_1_), channel_id=1, source_target_pairs={{0,7},{1,6},{2,5},{3,4},{4,3},{5,2},{6,1},{7,0},{8,15},{9,14},{10,... | collective-permute-start | bytes 196616 | tf_op jit(solution)/shard_map/ppermute | solution.py:562
